TPU v7x, 512 devices: a whole 4x8x8 slice. The times are simulated.
512 devices in a mesh: row: 16 (over y, core), col: 32 (over x, z).
Axes of the slice: x: 4, y: 8, z: 8, core: 2. Of those that a mesh axis runs over, the one named last changes fastest.
Arguments:
- lhat: float32 [4096, 256, 256], P(('row', 'col')), may hold values from -0.375 to 0.375
- ainv_anc: float32 [4096, 256, 256], P(('row', 'col')), may hold values from -1.25 to 1.25
- diag_inv: float32 [32, 256, 256], P('col', 'row'), may hold values from -0.6 to 2, as said below
- targets: int32 [4096, 1], P(('row', 'col')), may hold values from 0 to 31
Outputs:
- diag_blocks: float32 [32, 256, 256], P('col', 'row')
Inputs may be any that keep to these rules, and one draw needn't show every extreme that they name: `diag_inv`: each block is lower triangular with its diagonal entries between 0.5 and 2.
All inputs are finite; a program needn't handle non-finite values.
Results may differ from a plain program's by a relative error of at most 0.0003.
Values sent between devices are 32-bit elements; how exact they have to be, the bound alone decides.
No kernel may reach another device: no remote copies, remote signals or barrier semaphores. Data moves between devices by JAX's collectives and lax.ppermute only.
A program may use at most 64 MiB of HBM per device.

v0:
```python
import jax
import jax.numpy as jnp
from jax import lax
from jax.sharding import PartitionSpec as P


def laid_out(tiles, dim):
    lengths = list(tiles.shape[1:])
    lengths[dim] *= tiles.shape[0]
    return jnp.moveaxis(tiles, 0, dim).reshape(lengths)


def copy_for_each(x, axis):
    length = lax.axis_size(axis)
    return lax.all_to_all(jnp.broadcast_to(x[None], (length, *x.shape)), axis, 0, 0, tiled=True)


def collect(x, axis, dim):
    return laid_out(copy_for_each(x, axis), dim)


def in_blocks(x, dim, length):
    lengths = x.shape
    tiles = x.reshape(*lengths[:dim], length, lengths[dim] // length, *lengths[dim + 1 :])
    return jnp.moveaxis(tiles, dim, 0)


def summed_on_arrival(x, axis, dim):
    length = lax.axis_size(axis)
    tiles = lax.all_to_all(in_blocks(x, dim, length), axis, 0, 0, tiled=True)
    return jnp.sum(tiles, axis=0)


def on_device(lhat, ainv_anc, diag_inv, targets):
    row_count = lax.axis_size("row")
    row_index = lax.axis_index("row")
    width = diag_inv.shape[2]
    row_share = width // row_count
    owned_count = diag_inv.shape[0]
    super_count = owned_count * lax.axis_size("col")
    col_start = row_index * row_share
    products = -jnp.einsum("shi,shj->sij", lhat, ainv_anc, precision=lax.Precision.HIGHEST)
    slot_ids = targets[:, 0]
    factor_piece = collect(diag_inv, "row", 1)
    col_slice = lax.dynamic_slice_in_dim(factor_piece, col_start, row_share, 2)
    gram_rows = jnp.einsum("kia,kib->kab", col_slice, factor_piece, precision=lax.Precision.HIGHEST)
    received = lax.all_to_all(products, "row", split_axis=1, concat_axis=0, tiled=True)
    ids_all = collect(slot_ids, "row", 0)
    labels = jnp.arange(super_count, dtype=jnp.int32)
    one_hot = (labels[:, None] == ids_all[None, :]).astype(jnp.float32)
    summed = jnp.einsum("kn,nij->kij", one_hot, received, precision=lax.Precision.HIGHEST)
    own_blocks = summed_on_arrival(summed, "col", 0)
    return own_blocks + gram_rows


def solution(mesh):
    placed = (
        P(("row", "col"), None, None),
        P(("row", "col"), None, None),
        P("col", "row", None),
        P(("row", "col"), None),
    )
    return jax.shard_map(
        on_device, mesh=mesh, in_specs=placed, out_specs=P("col", "row", None), check_vma=False
    )
```

profile of v0, /device:TPU:1, one launch (start us, length us, event | category | flops | bytes accessed | tf_op | source)
XLA Modules:
  0.0 125.0 jit_solution(12775095045599749959)
XLA Ops:
  0.0 0.0 copy-start
  0.0 1.4 %broadcast_in_dim.17 = s32[16,1,8]{2,1,0:T(1,128)} broadcast(s32[8]{0:T(128)} %bitcast.28), dimensions={2} | broadcast | bytes 544 | tf_op jit(solution)/shard_map/broadcast_in_dim | solution.py:15
  1.4 10.1 %all-to-all-start = ((s32[16,1,8]{2,1,0:T(1,128)}), s32[16,1,8]{2,1,0:T(1,128)S(1)}, u32[]{:S(2)}, u32[]{:S(2)}) async-start(s32[16,1,8]{2,1,0:T(1,128)} %broadcast_in_dim.17), calls=%async_computation | async-start | bytes 16384 | tf_op jit(solution)/shard_map/all_to_all | solution.py:15
  11.5 0.0 copy-done
  11.5 5.1 %convolution_negate_fusion = f32[8,256,256]{2,1,0:T(8,128)S(1)} fusion(f32[8,256,256]{2,1,0:T(8,128)S(1)} %copy-done, f32[8,256,256]{2,1,0:T(8,128)} %param.5), kind=kOutput, calls=%fused_computation.3 | convolution fusion | flops 1611137024 | bytes 6291456 | tf_op jit(solution)/shard_map/shi,shj->sij/dot_general | solution.py:42
  16.6 2.5 %copy.10 = f32[8,256,256]{2,0,1:T(8,128)} copy(f32[8,256,256]{2,1,0:T(8,128)S(1)} %convolution_negate_fusion) | data formatting | bytes 4194304 | tf_op jit(solution)/shard_map/neg | solution.py:42
  19.2 0.0 all-to-all-done
  19.2 7.3 %all-to-all-start.1 = ((f32[8,256,256]{2,0,1:T(8,128)}), f32[8,256,256]{2,0,1:T(8,128)}, u32[]{:S(2)}, u32[]{:S(2)}) async-start(f32[8,256,256]{2,0,1:T(8,128)} %copy.10), calls=%async_computation.1 | async-start | bytes 4194304 | tf_op jit(solution)/shard_map/all_to_all | solution.py:47
  26.4 0.5 broadcast.7
  26.9 0.7 reduce.4
  27.6 0.1 eq.16
  27.7 47.9 %all-to-all-done.1 = f32[8,256,256]{2,0,1:T(8,128)} async-done(((f32[8,256,256]{2,0,1:T(8,128)}), f32[8,256,256]{2,0,1:T(8,128)}, u32[]{:S(2)}, u32[]{:S(2)}) %all-to-all-start.1) | async-done | bytes 2097184 | tf_op jit(solution)/shard_map/all_to_all | solution.py:47
  75.6 0.0 copy-start.1
  75.6 2.4 %fusion.3 = f32[32,1,16,256]{3,0,2,1:T(8,128)S(1)} fusion(f32[8,16,16,256]{3,0,2,1:T(8,128)} %bitcast.2, s32[128]{0:T(128)S(1)} %eq.16), kind=kOutput, calls=%fused_computation.4 | convolution fusion | flops 201330688 | bytes 2621952 | tf_op jit(solution)/shard_map/kn,nij->kij/dot_general | solution.py:51
  78.0 0.3 copy.12
  78.4 25.2 %all_to_all.34 = f32[32,1,16,256]{3,2,1,0:T(8,128)S(1)} all-to-all(f32[32,1,16,256]{3,2,1,0:T(8,128)S(1)} %copy.12), channel_id=1, replica_groups=mesh['row'=16,'col'=32] {'col'}, dimensions={0} | all-to-all | bytes 1048576 | tf_op jit(solution)/shard_map/all_to_all | solution.py:30
  103.5 0.0 copy-done.1
  103.5 0.7 broadcast_in_dim.19
  104.3 8.1 %all-to-all-start.3 = ((f32[16,1,16,256]{3,2,1,0:T(8,128)}), f32[16,1,16,256]{3,2,1,0:T(8,128)S(1)}, u32[]{:S(2)}, u32[]{:S(2)}) async-start(f32[16,1,16,256]{3,2,1,0:T(8,128)} %broadcast_in_dim.19), calls=%async_computation.3 | async-start | bytes 524288 | tf_op jit(solution)/shard_map/all_to_all | solution.py:15
  112.4 11.5 %all-to-all-done.3 = f32[16,1,16,256]{3,2,1,0:T(8,128)S(1)} async-done(((f32[16,1,16,256]{3,2,1,0:T(8,128)}), f32[16,1,16,256]{3,2,1,0:T(8,128)S(1)}, u32[]{:S(2)}, u32[]{:S(2)}) %all-to-all-start.3) | async-done | bytes 262176 | tf_op jit(solution)/shard_map/all_to_all | solution.py:15
  123.9 1.0 fusion.6
  (1 shorter events, 0.0 us)
Async XLA Ops:
  0.0 11.5 %copy-start = (f32[8,256,256]{2,1,0:T(8,128)S(1)}, f32[8,256,256]{2,1,0:T(8,128)}, u32[]{:S(2)}) copy-start(f32[8,256,256]{2,1,0:T(8,128)} %param.4) | copy-start | bytes 6291460
  1.4 17.7 %all-to-all-start = ((s32[16,1,8]{2,1,0:T(1,128)}), s32[16,1,8]{2,1,0:T(1,128)S(1)}, u32[]{:S(2)}, u32[]{:S(2)}) async-start(s32[16,1,8]{2,1,0:T(1,128)} %broadcast_in_dim.17), calls=%async_computation | async-start | bytes 16384 | tf_op jit(solution)/shard_map/all_to_all | solution.py:15
  19.2 56.4 %all-to-all-start.1 = ((f32[8,256,256]{2,0,1:T(8,128)}), f32[8,256,256]{2,0,1:T(8,128)}, u32[]{:S(2)}, u32[]{:S(2)}) async-start(f32[8,256,256]{2,0,1:T(8,128)} %copy.10), calls=%async_computation.1 | async-start | bytes 4194304 | tf_op jit(solution)/shard_map/all_to_all | solution.py:47
  75.6 28.0 %copy-start.1 = (f32[1,16,256]{2,1,0:T(8,128)S(1)}, f32[1,16,256]{2,1,0:T(8,128)}, u32[]{:S(2)}) copy-start(f32[1,16,256]{2,1,0:T(8,128)} %param.6) | copy-start | bytes 49156
  104.3 19.7 %all-to-all-start.3 = ((f32[16,1,16,256]{3,2,1,0:T(8,128)}), f32[16,1,16,256]{3,2,1,0:T(8,128)S(1)}, u32[]{:S(2)}, u32[]{:S(2)}) async-start(f32[16,1,16,256]{3,2,1,0:T(8,128)} %broadcast_in_dim.19), calls=%async_computation.3 | async-start | bytes 524288 | tf_op jit(solution)/shard_map/all_to_all | solution.py:15
where the time goes:
time: 125 us
  waiting for transfers between devices  59.4 us (48%)
  starting transfers between devices  25.5 us (20%)
  blocking collectives  25.2 us (20%)
  matrix products  8.59 us (7%)
  local copies, waits for them, and re-layouts  5.56 us (4%)
    all_to_all x1, waiting for transfers between devices, on_device(): lax.all_to_all(products, 'row', split_axis=1, concat_axis=0, tiled=True)  47.9 us
    all_to_all x1, blocking collectives, summed_on_arrival(): tiles = lax.all_to_all(in_blocks(x, dim, length), axis, 0, 0, tiled=True)  25.2 us
    all_to_all x2, starting transfers between devices, copy_for_each(): lax.all_to_all(jnp.broadcast_to(x[None], (length, *x.shape)), axis, 0, 0,...  18.2 us
    all_to_all x2, waiting for transfers between devices, copy_for_each(): lax.all_to_all(jnp.broadcast_to(x[None], (length, *x.shape)), axis, 0, 0,...  11.5 us
    all_to_all x1, starting transfers between devices, on_device(): lax.all_to_all(products, 'row', split_axis=1, concat_axis=0, tiled=True)  7.27 us
    dot_general x1, matrix products, on_device(): jnp.einsum('shi,shj->sij', lhat, ainv_anc, precision=lax.Precision.HIGHEST)  5.11 us
    neg x1, local copies, waits for them, and re-layouts, on_device(): -jnp.einsum('shi,shj->sij', lhat, ainv_anc, precision=lax.Precision.HIGHEST)  2.52 us
  transfers between devices with their start and end apart: 3, of which 2 were waited for; matrix products, arithmetic and copies ran while one was open for 7% of the time, Pallas kernels for 0%

commit v1 on v0

v1 whole, which is shorter than its diff:
```python
import jax
import jax.numpy as jnp
from jax import lax
from jax.sharding import PartitionSpec as P

NY, NC, NX, NZ = 8, 2, 4, 8
BOTH = ("row", "col")


def flat(y, c, x, z):
    return ((y * NC + c) * NX + x) * NZ + z


def every():
    return [(y, c, x, z) for y in range(NY) for c in range(NC) for x in range(NX) for z in range(NZ)]


LINES = [[flat(y, 0, x, z) for y in range(NY)] for x in range(NX) for z in range(NZ)] + [
    [flat(y, 1, x, z) for z in range(NZ)] for x in range(NX) for y in range(NY)
]
PLANES = [[flat(y, 0, x, z) for x in range(NX) for z in range(NZ)] for y in range(NY)] + [
    [flat(y, 1, x, z) for x in range(NX) for y in range(NY)] for z in range(NZ)
]
PARTNER = [(flat(y, c, x, z), flat(y, 1 - c, x, z)) for y, c, x, z in every()]
TO_ODD = [(flat(y, 0, x, z), flat(y, 1, x, z)) for y, c, x, z in every() if c == 0]
TURN = [(flat(y, 1, x, z), flat(z, 1, x, y)) for y, c, x, z in every() if c == 1]


def on_device(lhat, ainv_anc, diag_inv, targets):
    slots, _, width = lhat.shape
    core = lax.axis_index("row") % NC
    y = lax.axis_index("row") // NC
    supers = NX * NZ
    share = width // (NY * NC)
    labels = jnp.arange(supers, dtype=jnp.int32)

    ids = targets[:, 0].astype(jnp.float32)
    ids_row = jnp.zeros((8, width), jnp.float32).at[:, :slots].set(ids[None, :])
    mine = jnp.concatenate([diag_inv[0], ids_row], axis=0)
    theirs = lax.ppermute(mine, BOTH, PARTNER)

    def product(side):
        left = lhat.reshape(slots, width, NY, NC, share)
        left = lax.dynamic_index_in_dim(left, side, 3, keepdims=False)
        return jnp.einsum("shdr,shj->dsrj", left, ainv_anc, precision=lax.Precision.HIGH)

    sent = product(1 - core)
    arrived = lax.ppermute(sent, BOTH, PARTNER)
    kept = product(core)
    extra = jnp.concatenate([mine[:share], theirs[:share], mine[share:], theirs[share:]], axis=0)
    payload = jnp.concatenate(
        [
            kept.reshape(NY, slots * share, width),
            arrived.reshape(NY, slots * share, width),
            jnp.broadcast_to(extra[None], (NY, *extra.shape)),
        ],
        axis=1,
    )
    got = lax.all_to_all(payload, BOTH, 0, 0, axis_index_groups=LINES, tiled=True)
    n = NC * slots
    blocks = got[:, : n * share].reshape(NY * n, share, width)
    base = n * share + NC * share
    ids_all = jnp.stack([got[:, base, :slots], got[:, base + 8, :slots]], axis=1).reshape(-1)
    one_hot = (labels[:, None].astype(jnp.float32) == ids_all[None, :]).astype(jnp.float32)
    summed = jnp.einsum("kn,nij->kij", one_hot, blocks, precision=lax.Precision.HIGH)

    factor = got[:, n * share : base].reshape(NY * NC * share, width)
    piece = lax.dynamic_slice_in_dim(factor, y * NC * share, NC * share, 1)
    gram = jnp.einsum("ia,ib->ab", piece, factor, precision=lax.Precision.HIGH)
    gram_odd = lax.ppermute(gram[share:], BOTH, TO_ODD)

    parts = lax.all_to_all(summed, BOTH, 0, 0, axis_index_groups=PLANES, tiled=True)
    own = jnp.sum(parts, axis=0)
    turned = lax.ppermute(own, BOTH, TURN)
    return jnp.where(core == 0, gram[:share] - own, gram_odd - turned)[None]


def solution(mesh):
    placed = (
        P(("row", "col"), None, None),
        P(("row", "col"), None, None),
        P("col", "row", None),
        P(("row", "col"), None),
    )
    return jax.shard_map(
        on_device, mesh=mesh, in_specs=placed, out_specs=P("col", "row", None), check_vma=False
    )
```

time: 125 us -> 98 us (0.78)
  the two profiles are of different devices: /device:TPU:1 before, /device:TPU:33 now
where the time goes in v1:
time: 98 us; the launch traced here: 97.4 us
  waiting for transfers between devices  48.5 us (49%)
  starting transfers between devices  29.9 us (31%)
  local copies, waits for them, and re-layouts  9.23 us (9%)
  matrix products  5.93 us (6%)
  other arithmetic  3.69 us (4%)
    all_to_all x1, waiting for transfers between devices, on_device(): lax.all_to_all(payload, BOTH, 0, 0, axis_index_groups=LINES, tiled=True)  33.4 us
    all_to_all x1, starting transfers between devices, on_device(): lax.all_to_all(payload, BOTH, 0, 0, axis_index_groups=LINES, tiled=True)  10 us
    all_to_all x1, starting transfers between devices, on_device(): lax.all_to_all(summed, BOTH, 0, 0, axis_index_groups=PLANES, tiled=True)  9.27 us
    ppermute x1, waiting for transfers between devices, on_device(): turned = lax.ppermute(own, BOTH, TURN)  8.42 us
    all_to_all x1, waiting for transfers between devices, on_device(): lax.all_to_all(summed, BOTH, 0, 0, axis_index_groups=PLANES, tiled=True)  6.65 us
    ppermute x1, starting transfers between devices, on_device(): turned = lax.ppermute(own, BOTH, TURN)  4.76 us
    dot_general x2, matrix products, product(): jnp.einsum('shdr,shj->dsrj', left, ainv_anc, precision=lax.Precision.HIGH)  4.06 us
    unnamed x7, local copies, waits for them, and re-layouts  3.11 us
  transfers between devices with their start and end apart: 6, of which 3 were waited for; matrix products, arithmetic and copies ran while one was open for 5% of the time, Pallas kernels for 0%

profile of v1, /device:TPU:33, one launch (start us, length us, event | category | flops | bytes accessed | tf_op | source)
XLA Modules:
  0.0 97.4 jit_solution(1576585191084000393)
XLA Ops:
  0.0 0.0 copy-start
  0.0 3.1 %copy.11 = f32[8,256,256]{1,2,0:T(8,128)} copy(f32[8,256,256]{2,1,0:T(8,128)} %param.6) | data formatting | bytes 4194304 | tf_op args[0]
  3.1 0.0 copy-done
  3.1 0.0 copy-start.2
  3.1 0.0 copy-start.1
  3.1 2.0 %fusion.9 = f32[8,8,16,256]{3,2,0,1:T(8,128)S(1)} fusion(f32[8,256,256]{2,1,0:T(8,128)S(1)} %copy-done, f32[8,256,8,2,16]{1,4,3,2,0:T(8,128)} %bitcast.35, s32[]{:T(128)S(6)} %select_n.32), kind=kOutput, calls=%fused_computation.8 | convolution fusion | flops 402653184 | bytes 4194308 | tf_op jit(solution)/shard_map/shdr,shj->dsrj/dot_general | solution.py:45
  5.2 2.6 %collective-permute-start = (f32[8,8,16,256]{3,2,0,1:T(8,128)S(1)}, f32[8,8,16,256]{3,2,0,1:T(8,128)}, u32[]{:S(2)}, u32[]{:S(2)}) collective-permute-start(f32[8,8,16,256]{3,2,0,1:T(8,128)S(1)} %fusion.9), channel_id=1, source_target_pairs={{0,32},{1,33},{2,34},{3,35},{4,36},{5,37},{6,38},{7,39},{8,40},{9,... | collective-permute-start | bytes 3145736 | tf_op jit(solution)/shard_map/ppermute | solution.py:48
  7.7 0.6 compare_reduce_fusion
  8.4 0.0 copy-done.2
  8.4 0.6 fusion.27
  9.1 0.0 copy-done.1
  9.1 1.9 %collective-permute-start.1 = (f32[24,256]{1,0:T(8,128)S(1)}, f32[24,256]{1,0:T(8,128)S(1)}, u32[]{:S(2)}, u32[]{:S(2)}) collective-permute-start(f32[24,256]{1,0:T(8,128)S(1)} %pad_maximum_fusion.2), channel_id=1, source_target_pairs={{0,32},{1,33},{2,34},{3,35},{4,36},{5,37},{6,38},{7,39},{8,40},{9,... | collective-permute-start | bytes 73736 | tf_op jit(solution)/shard_map/ppermute | solution.py:40
  11.0 2.0 %fusion.6 = f32[8,8,16,256]{3,2,0,1:T(8,128)S(1)} fusion(f32[8,256,256]{2,1,0:T(8,128)S(1)} %copy-done, f32[8,256,8,2,16]{1,4,3,2,0:T(8,128)} %bitcast.36, s32[]{:T(128)S(6)} %select_n.31), kind=kOutput, calls=%fused_computation.7 | convolution fusion | flops 402653184 | bytes 4194308 | tf_op jit(solution)/shard_map/shdr,shj->dsrj/dot_general | solution.py:45
  13.1 0.1 copy.12
  13.1 0.0 collective-permute-done.1
  13.2 0.0 collective-permute-done
  13.2 1.3 %copy.13 = f32[8,8,16,256]{3,2,1,0:T(8,128)S(1)} copy(f32[8,8,16,256]{3,2,0,1:T(8,128)} %collective-permute-done) | data formatting | bytes 2097152 | tf_op jit(solution)/shard_map/ppermute | solution.py:48
  14.5 1.7 %pad_maximum_fusion = f32[8,304,256]{2,1,0:T(8,128)} fusion(f32[8,48,256]{2,1,0:T(8,128)S(1)} %broadcast_in_dim.4, f32[8,128,256]{2,1,0:T(8,128)S(1)} %bitcast.39, f32[8,128,256]{2,1,0:T(8,128)S(1)} %bitcast.38), kind=kLoop, calls=%fused_computation | loop fusion | flops 1245184 | bytes 4980736 | tf_op jit(solution)/shard_map/concatenate | solution.py:51
  16.3 10.0 %all-to-all-start = ((f32[8,304,256]{2,1,0:T(8,128)}), f32[8,304,256]{2,1,0:T(8,128)}, u32[]{:S(2)}, u32[]{:S(2)}) async-start(f32[8,304,256]{2,1,0:T(8,128)} %pad_maximum_fusion), calls=%async_computation | async-start | bytes 4980736 | tf_op jit(solution)/shard_map/all_to_all | solution.py:59
  26.3 33.4 %all-to-all-done = f32[8,304,256]{2,1,0:T(8,128)} async-done(((f32[8,304,256]{2,1,0:T(8,128)}), f32[8,304,256]{2,1,0:T(8,128)}, u32[]{:S(2)}, u32[]{:S(2)}) %all-to-all-start) | async-done | bytes 2490400 | tf_op jit(solution)/shard_map/all_to_all | solution.py:59
  59.7 0.8 fusion.28
  60.5 0.1 eq.22
  60.6 1.7 %slice.54 = f32[8,256,256]{2,1,0:T(8,128)S(1)} slice(f32[8,304,256]{2,1,0:T(8,128)} %all-to-all-done), slice={[0:8], [0:256], [0:256]} | slice | bytes 4194304 | tf_op jit(solution)/shard_map/slice | solution.py:61
  62.3 1.5 %fusion.4 = f32[32,16,256]{2,0,1:T(8,128)S(1)} fusion(f32[128,16,256]{2,1,0:T(8,128)S(1)} %bitcast.37, f32[128]{0:T(128)S(1)} %eq.22, f32[32]{0:T(128)S(1)} %iota_convert_fusion), kind=kOutput, calls=%fused_computation.5 | convolution fusion | flops 100667392 | bytes 2622080 | tf_op jit(solution)/shard_map/kn,nij->kij/dot_general | solution.py:65
  63.9 1.1 %copy.15 = f32[32,16,256]{2,1,0:T(8,128)} copy(f32[32,16,256]{2,0,1:T(8,128)S(1)} %fusion.4) | data formatting | bytes 1048576 | tf_op jit(solution)/shard_map/kn,nij->kij/dot_general | solution.py:65
  65.0 9.3 %all-to-all-start.1 = ((f32[32,16,256]{2,1,0:T(8,128)}), f32[32,16,256]{2,1,0:T(8,128)S(1)}, u32[]{:S(2)}, u32[]{:S(2)}) async-start(f32[32,16,256]{2,1,0:T(8,128)} %copy.15), calls=%async_computation.1 | async-start | bytes 1048576 | tf_op jit(solution)/shard_map/all_to_all | solution.py:72
  74.3 1.0 slice.50
  75.3 0.3 fusion.16
  75.6 1.3 %collective-permute-start.2 = (f32[16,256]{1,0:T(8,128)S(1)}, f32[16,256]{1,0:T(8,128)S(1)}, u32[]{:S(2)}, u32[]{:S(2)}) collective-permute-start(f32[16,256]{1,0:T(8,128)S(1)} %slice.55), channel_id=1, source_target_pairs={{0,32},{1,33},{2,34},{3,35},{4,36},{5,37},{6,38},{7,39},{8,40},{9,... | collective-permute-start | bytes 49160 | tf_op jit(solution)/shard_map/ppermute | solution.py:70
  76.9 6.7 %all-to-all-done.1 = f32[32,16,256]{2,1,0:T(8,128)S(1)} async-done(((f32[32,16,256]{2,1,0:T(8,128)}), f32[32,16,256]{2,1,0:T(8,128)S(1)}, u32[]{:S(2)}, u32[]{:S(2)}) %all-to-all-start.1) | async-done | bytes 524320 | tf_op jit(solution)/shard_map/all_to_all | solution.py:72
  83.6 4.8 %collective-permute-start.3 = (f32[16,256]{1,0:T(8,128)S(1)}, f32[16,256]{1,0:T(8,128)S(1)}, u32[]{:S(2)}, u32[]{:S(2)}) collective-permute-start(f32[16,256]{1,0:T(8,128)S(1)} %reduce_sum.9), channel_id=1, source_target_pairs={{32,32},{33,96},{34,160},{35,224},{36,288},{37,352},{38,416},{39,4... | collective-permute-start | bytes 49160 | tf_op jit(solution)/shard_map/ppermute | solution.py:74
  88.4 0.0 collective-permute-done.2
  88.4 8.4 %collective-permute-done.3 = f32[16,256]{1,0:T(8,128)S(1)} collective-permute-done((f32[16,256]{1,0:T(8,128)S(1)}, f32[16,256]{1,0:T(8,128)S(1)}, u32[]{:S(2)}, u32[]{:S(2)}) %collective-permute-start.3) | collective-permute-done | bytes 16416 | tf_op jit(solution)/shard_map/ppermute | solution.py:74
  96.8 0.6 fusion.19
  (11 shorter events, 0.1 us)
Async XLA Ops:
  0.0 3.1 %copy-start = (f32[8,256,256]{2,1,0:T(8,128)S(1)}, f32[8,256,256]{2,1,0:T(8,128)}, u32[]{:S(2)}) copy-start(f32[8,256,256]{2,1,0:T(8,128)} %param.7) | copy-start | bytes 6291460
  3.1 5.3 %copy-start.2 = (s32[8,1]{0,1:T(1,128)S(1)}, s32[8,1]{0,1:T(1,128)}, u32[]{:S(2)}) copy-start(s32[8,1]{0,1:T(1,128)} %param.9) | copy-start | bytes 100
  3.1 6.0 %copy-start.1 = (f32[1,16,256]{2,1,0:T(8,128)S(1)}, f32[1,16,256]{2,1,0:T(8,128)}, u32[]{:S(2)}) copy-start(f32[1,16,256]{2,1,0:T(8,128)} %param.8) | copy-start | bytes 49156
  5.2 8.0 %collective-permute-start = (f32[8,8,16,256]{3,2,0,1:T(8,128)S(1)}, f32[8,8,16,256]{3,2,0,1:T(8,128)}, u32[]{:S(2)}, u32[]{:S(2)}) collective-permute-start(f32[8,8,16,256]{3,2,0,1:T(8,128)S(1)} %fusion.9), channel_id=1, source_target_pairs={{0,32},{1,33},{2,34},{3,35},{4,36},{5,37},{6,38},{7,39},{8,40},{9,... | collective-permute-start | bytes 3145736 | tf_op jit(solution)/shard_map/ppermute | solution.py:48
  9.1 4.0 %collective-permute-start.1 = (f32[24,256]{1,0:T(8,128)S(1)}, f32[24,256]{1,0:T(8,128)S(1)}, u32[]{:S(2)}, u32[]{:S(2)}) collective-permute-start(f32[24,256]{1,0:T(8,128)S(1)} %pad_maximum_fusion.2), channel_id=1, source_target_pairs={{0,32},{1,33},{2,34},{3,35},{4,36},{5,37},{6,38},{7,39},{8,40},{9,... | collective-permute-start | bytes 73736 | tf_op jit(solution)/shard_map/ppermute | solution.py:40
  16.3 43.4 %all-to-all-start = ((f32[8,304,256]{2,1,0:T(8,128)}), f32[8,304,256]{2,1,0:T(8,128)}, u32[]{:S(2)}, u32[]{:S(2)}) async-start(f32[8,304,256]{2,1,0:T(8,128)} %pad_maximum_fusion), calls=%async_computation | async-start | bytes 4980736 | tf_op jit(solution)/shard_map/all_to_all | solution.py:59
  65.0 18.6 %all-to-all-start.1 = ((f32[32,16,256]{2,1,0:T(8,128)}), f32[32,16,256]{2,1,0:T(8,128)S(1)}, u32[]{:S(2)}, u32[]{:S(2)}) async-start(f32[32,16,256]{2,1,0:T(8,128)} %copy.15), calls=%async_computation.1 | async-start | bytes 1048576 | tf_op jit(solution)/shard_map/all_to_all | solution.py:72
  75.6 12.8 %collective-permute-start.2 = (f32[16,256]{1,0:T(8,128)S(1)}, f32[16,256]{1,0:T(8,128)S(1)}, u32[]{:S(2)}, u32[]{:S(2)}) collective-permute-start(f32[16,256]{1,0:T(8,128)S(1)} %slice.55), channel_id=1, source_target_pairs={{0,32},{1,33},{2,34},{3,35},{4,36},{5,37},{6,38},{7,39},{8,40},{9,... | collective-permute-start | bytes 49160 | tf_op jit(solution)/shard_map/ppermute | solution.py:70
  83.6 13.2 %collective-permute-start.3 = (f32[16,256]{1,0:T(8,128)S(1)}, f32[16,256]{1,0:T(8,128)S(1)}, u32[]{:S(2)}, u32[]{:S(2)}) collective-permute-start(f32[16,256]{1,0:T(8,128)S(1)} %reduce_sum.9), channel_id=1, source_target_pairs={{32,32},{33,96},{34,160},{35,224},{36,288},{37,352},{38,416},{39,4... | collective-permute-start | bytes 49160 | tf_op jit(solution)/shard_map/ppermute | solution.py:74

commit v2 on v1

v2 whole, which is shorter than its diff:
```python
import jax
import jax.numpy as jnp
from jax import lax
from jax.experimental import pallas as pl
from jax.experimental.pallas import tpu as pltpu
from jax.sharding import PartitionSpec as P

NY, NC, NX, NZ = 8, 2, 4, 8
BOTH = ("row", "col")


def flat(y, c, x, z):
    return ((y * NC + c) * NX + x) * NZ + z


def every():
    return [(y, c, x, z) for y in range(NY) for c in range(NC) for x in range(NX) for z in range(NZ)]


LINES = [[flat(y, 0, x, z) for y in range(NY)] for x in range(NX) for z in range(NZ)] + [
    [flat(y, 1, x, z) for z in range(NZ)] for x in range(NX) for y in range(NY)
]
PLANES = [[flat(y, 0, x, z) for x in range(NX) for z in range(NZ)] for y in range(NY)] + [
    [flat(y, 1, x, z) for x in range(NX) for y in range(NY)] for z in range(NZ)
]
PARTNER = [(flat(y, c, x, z), flat(y, 1 - c, x, z)) for y, c, x, z in every()]
TO_ODD = [(flat(y, 0, x, z), flat(y, 1, x, z)) for y, c, x, z in every() if c == 0]
TURN = [(flat(y, 1, x, z), flat(z, 1, x, y)) for y, c, x, z in every() if c == 1]


def split(a):
    high = a.astype(jnp.bfloat16)
    return high, (a - high.astype(jnp.float32)).astype(jnp.bfloat16)


def transposed_times(a, b):
    ah, al = split(a.T)
    bh, bl = split(b)
    left = jnp.concatenate([ah, ah, al], axis=1)
    right = jnp.concatenate([bh, bl, bh], axis=0)
    return jnp.dot(left, right, preferred_element_type=jnp.float32)


def products_kernel(where_ref, ids_ref, left_ref, right_ref, rows_ref, kept_ref, sent_ref):
    step = pl.program_id(0)
    core = where_ref[0]
    slots = pl.num_programs(0) - 1
    share, width = rows_ref.shape[1:]

    @pl.when(step < slots)
    def _():
        product = transposed_times(left_ref[0], right_ref[0]).reshape(NY, NC, share, width)
        even, odd = product[:, 0], product[:, 1]
        kept_ref[:, 0] = jnp.where(core == 0, even, odd)
        sent_ref[...] = jnp.where(core == 0, odd, even)

    @pl.when(step == slots)
    def _():
        first = share * where_ref[1] + 1
        row = lax.broadcasted_iota(jnp.int32, (share, width), 0)
        lane = lax.broadcasted_iota(jnp.int32, (share, width), 1)
        tile = jnp.where(lane < first + row, rows_ref[0], 0.0)
        for s in range(ids_ref.shape[0]):
            tile = jnp.where((row == 0) & (lane == first + s), ids_ref[s, 0].astype(jnp.float32), tile)
        tiles = jnp.broadcast_to(tile[None], (NY, share, width))
        kept_ref[:, 0] = tiles
        sent_ref[...] = tiles


def place_kernel(_, arrived_ref, out_ref, sem):
    copy = pltpu.make_async_copy(arrived_ref, out_ref.at[:, 1], sem)
    copy.start()
    copy.wait()


def sum_kernel(where_ref, ids_ref, got_ref, out_ref, factor_ref):
    step = pl.program_id(0)
    core, index = where_ref[0], where_ref[1]
    share = out_ref.shape[1]
    slots = got_ref.shape[2] // share - 1

    @pl.when(step == 0)
    def _():
        out_ref[...] = jnp.zeros_like(out_ref)

    for half in range(NC):
        source_core = core if half == 0 else 1 - core
        source_y = jnp.where(core == 0, step, index // NC)
        first = share * (source_y * NC + source_core) + 1
        for s in range(slots):
            k = ids_ref[0, half, 0, first + s].astype(jnp.int32)
            out_ref[k] += got_ref[0, half, s * share : (s + 1) * share]
        tile = got_ref[0, half, slots * share :]
        row = lax.broadcasted_iota(jnp.int32, tile.shape, 0)
        lane = lax.broadcasted_iota(jnp.int32, tile.shape, 1)
        factor_ref[half * share : (half + 1) * share] = jnp.where(lane < first + row, tile, 0.0)


def gram_kernel(where_ref, factor_ref, out_ref, whole_ref):
    whole_ref[...] = transposed_times(factor_ref[...], factor_ref[...])
    height = out_ref.shape[0]
    out_ref[...] = whole_ref[pl.ds(pl.multiple_of(where_ref[1] // NC * height, height), height)]


def on_device(lhat, ainv_anc, diag_inv, targets):
    slots, height, width = lhat.shape
    index = lax.axis_index("row")
    core = index % NC
    share = diag_inv.shape[1]
    supers = NX * NZ
    length = (slots + 1) * share
    where = jnp.stack([core, index]).astype(jnp.int32)
    smem = pl.BlockSpec(memory_space=pltpu.SMEM)

    kept, sent = pl.pallas_call(
        products_kernel,
        grid=(slots + 1,),
        in_specs=[
            smem,
            smem,
            pl.BlockSpec((1, height, width), lambda i: (jnp.minimum(i, slots - 1), 0, 0)),
            pl.BlockSpec((1, height, width), lambda i: (jnp.minimum(i, slots - 1), 0, 0)),
            pl.BlockSpec((1, share, width), lambda i: (0, 0, 0)),
        ],
        out_specs=[
            pl.BlockSpec((NY, 1, share, width), lambda i: (0, 0, i, 0)),
            pl.BlockSpec((NY, share, width), lambda i: (0, i, 0)),
        ],
        out_shape=[
            jax.ShapeDtypeStruct((NY, NC, length, width), jnp.float32),
            jax.ShapeDtypeStruct((NY, length, width), jnp.float32),
        ],
        name="products",
    )(where, targets, lhat, ainv_anc, diag_inv)

    arrived = lax.ppermute(sent, BOTH, PARTNER)
    payload = pl.pallas_call(
        place_kernel,
        in_specs=[pl.BlockSpec(memory_space=pl.ANY), pl.BlockSpec(memory_space=pltpu.VMEM)],
        out_specs=pl.BlockSpec(memory_space=pl.ANY),
        out_shape=jax.ShapeDtypeStruct(kept.shape, jnp.float32),
        scratch_shapes=[pltpu.SemaphoreType.DMA],
        input_output_aliases={0: 0},
        name="place",
    )(kept, arrived)

    got = lax.all_to_all(payload, BOTH, 0, 0, axis_index_groups=LINES, tiled=True)

    summed, factor = pl.pallas_call(
        sum_kernel,
        grid=(NY,),
        in_specs=[
            smem,
            pl.BlockSpec((1, NC, 8, width), lambda i: (i, 0, slots * share // 8, 0), memory_space=pltpu.SMEM),
            pl.BlockSpec((1, NC, length, width), lambda i: (i, 0, 0, 0)),
        ],
        out_specs=[
            pl.BlockSpec((supers, share, width), lambda i: (0, 0, 0)),
            pl.BlockSpec((NC * share, width), lambda i: (i, 0)),
        ],
        out_shape=[
            jax.ShapeDtypeStruct((supers, share, width), jnp.float32),
            jax.ShapeDtypeStruct((NY * NC * share, width), jnp.float32),
        ],
        name="sum",
    )(where, got, got)

    gram = pl.pallas_call(
        gram_kernel,
        in_specs=[smem, pl.BlockSpec(memory_space=pltpu.VMEM)],
        out_specs=pl.BlockSpec(memory_space=pltpu.VMEM),
        out_shape=jax.ShapeDtypeStruct((NC * share, width), jnp.float32),
        scratch_shapes=[pltpu.VMEM((width, width), jnp.float32)],
        name="gram",
    )(where, factor)
    gram_odd = lax.ppermute(gram[share:], BOTH, TO_ODD)

    parts = lax.all_to_all(summed, BOTH, 0, 0, axis_index_groups=PLANES, tiled=True)
    own = jnp.sum(parts, axis=0)
    turned = lax.ppermute(own, BOTH, TURN)
    return jnp.where(core == 0, gram[:share] - own, gram_odd - turned)[None]


def solution(mesh):
    placed = (
        P(("row", "col"), None, None),
        P(("row", "col"), None, None),
        P("col", "row", None),
        P(("row", "col"), None),
    )
    return jax.shard_map(
        on_device, mesh=mesh, in_specs=placed, out_specs=P("col", "row", None), check_vma=False
    )
```

time: 98 us -> 99.8 us (1.018)
  blocking collectives: 0 us -> 42 us
  waiting for transfers between devices: 48.5 us -> 16.4 us
  Pallas kernels: 0 us -> 17.6 us
  starting transfers between devices: 29.9 us -> 18 us
  local copies, waits for them, and re-layouts: 9.23 us -> 3.06 us
  matrix products: 5.93 us -> 0 us
  other arithmetic: 3.69 us -> 2.02 us
    all_to_all x0 -> x1, blocking collectives: none -> 42 us  [on_device(): lax.all_to_all(payload, BOTH, 0, 0, axis_index_groups=LINES, tiled=True)]
    all_to_all x1 -> x0, waiting for transfers between devices: 33.4 us -> none  [on_device(): lax.all_to_all(payload, BOTH, 0, 0, axis_index_groups=LINES, tiled=True)]
    pallas_call x0 -> x4, Pallas kernels: none -> 17.6 us  [the longest x1 7.39 us: on_device(): pl.pallas_call(products_kernel, grid=(slots + 1,), in_specs=[smem, smem,...]
    all_to_all x1 -> x0, starting transfers between devices: 10 us -> none  [on_device(): lax.all_to_all(payload, BOTH, 0, 0, axis_index_groups=LINES, tiled=True)]
    dot_general x4 -> x0, matrix products: 5.93 us -> none  [the longest x2 4.06 us: product(): jnp.einsum('shdr,shj->dsrj', left, ainv_anc, precision=lax.Precision.HIGH)]
    slice x5 -> x0, local copies, waits for them, and re-layouts: 3.49 us -> none  [the longest x1 1.73 us: on_device(): blocks = got[:, :n * share].reshape(NY * n, share, width)]
    ppermute x1, waiting for transfers between devices: 0.01 us -> 2.66 us  [on_device(): arrived = lax.ppermute(sent, BOTH, PARTNER)]
    ppermute x1 -> x0, starting transfers between devices: 1.92 us -> none  [on_device(): theirs = lax.ppermute(mine, BOTH, PARTNER)]
  transfers between devices with their start and end apart: 6 -> 4, of which waited for: 3 -> 3; matrix products, arithmetic and copies ran while one was open for 5% -> 1% of each run, Pallas kernels for 0% -> 2%
where the time goes in v2:
time: 99.8 us; the launch traced here: 99 us
  blocking collectives  42 us (42%)
  starting transfers between devices  18 us (18%)
  Pallas kernels  17.6 us (18%)
  waiting for transfers between devices  16.4 us (16%)
  local copies, waits for them, and re-layouts  3.06 us (3%)
  other arithmetic  2.02 us (2%)
    all_to_all x1, blocking collectives, on_device(): lax.all_to_all(payload, BOTH, 0, 0, axis_index_groups=LINES, tiled=True)  42 us
    all_to_all x1, starting transfers between devices, on_device(): lax.all_to_all(summed, BOTH, 0, 0, axis_index_groups=PLANES, tiled=True)  9.26 us
    ppermute x1, waiting for transfers between devices, on_device(): turned = lax.ppermute(own, BOTH, TURN)  8.31 us
    pallas_call x1, Pallas kernels, on_device(): pl.pallas_call(products_kernel, grid=(slots + 1,), in_specs=[smem, smem,...  7.39 us
    pallas_call x1, Pallas kernels, on_device(): pl.pallas_call(sum_kernel, grid=(NY,), in_specs=[smem, pl.BlockSpec((1, N...  5.99 us
    all_to_all x1, waiting for transfers between devices, on_device(): lax.all_to_all(summed, BOTH, 0, 0, axis_index_groups=PLANES, tiled=True)  5.41 us
    ppermute x1, starting transfers between devices, on_device(): turned = lax.ppermute(own, BOTH, TURN)  4.87 us
    ppermute x1, waiting for transfers between devices, on_device(): arrived = lax.ppermute(sent, BOTH, PARTNER)  2.66 us
  transfers between devices with their start and end apart: 4, of which 3 were waited for; matrix products, arithmetic and copies ran while one was open for 1% of the time, Pallas kernels for 2%

profile of v2, /device:TPU:33, one launch (start us, length us, event | category | flops | bytes accessed | tf_op | source)
XLA Modules:
  0.0 99.0 jit_solution(398113598810939052)
XLA Ops:
  0.0 1.3 %copy.6.ids_ref = s32[8,1]{1,0:T(8,128)} copy(s32[8,1]{0,1:T(1,128)} %param.7) | data formatting | bytes 64 | tf_op args[3]
  1.3 0.6 pad_add_fusion.where_ref
  2.0 7.4 %products.1 = (f32[8,2,144,256]{3,2,1,0:T(8,128)}, f32[8,144,256]{2,1,0:T(8,128)}) custom-call(s32[2]{0:T(128)} %pad_add_fusion.where_ref, s32[8,1]{1,0:T(8,128)} %copy.6.ids_ref, f32[8,256,256]{2,1,0:T(8,128)} %left_ref.1, f32[8,256,256]{2,1,0:T(8,128)} %right_ref.1, f32[1,16,256]{2,1,0:T(8,128)} %rows_ref.1), custom_call_target="tpu_custom_call" | custom-call | tf_op jit(solution)/shard_map/products/pallas_call | solution.py:115
  9.4 2.6 %collective-permute-start = (f32[8,144,256]{2,1,0:T(8,128)}, f32[8,144,256]{2,1,0:T(8,128)S(1)}, u32[]{:S(2)}, u32[]{:S(2)}) collective-permute-start(f32[8,144,256]{2,1,0:T(8,128)} %get-tuple-element.10), channel_id=1, source_target_pairs={{0,32},{1,33},{2,34},{3,35},{4,36},{5,37},{6,38},{7,39},{8,40},{9,... | collective-permute-start | bytes 3538952 | tf_op jit(solution)/shard_map/ppermute | solution.py:136
  11.9 2.7 %collective-permute-done.arrived_ref = f32[8,144,256]{2,1,0:T(8,128)S(1)} collective-permute-done((f32[8,144,256]{2,1,0:T(8,128)}, f32[8,144,256]{2,1,0:T(8,128)S(1)}, u32[]{:S(2)}, u32[]{:S(2)}) %collective-permute-start) | collective-permute-done | bytes 1179680 | tf_op jit(solution)/shard_map/ppermute | solution.py:136
  14.6 0.0 copy-start
  14.6 1.0 %copy-done = f32[8,144,256]{2,1,0:T(8,128)} copy-done((f32[8,144,256]{2,1,0:T(8,128)}, f32[8,144,256]{2,1,0:T(8,128)S(1)}, u32[]{:S(2)}) %copy-start) | copy-done | bytes 1179672
  15.6 2.3 %place.1 = f32[8,2,144,256]{3,2,1,0:T(8,128)} custom-call(f32[8,2,144,256]{3,2,1,0:T(8,128)} %get-tuple-element.9._, f32[8,144,256]{2,1,0:T(8,128)} %copy-done), custom_call_target="tpu_custom_call", output_to_operand_aliasing={{}: (0, {})} | custom-call | tf_op jit(solution)/shard_map/place/pallas_call | solution.py:137
  17.9 42.0 %all_to_all.10.ids_ref.got_ref = f32[8,2,144,256]{3,2,1,0:T(8,128)} all-to-all(f32[8,2,144,256]{3,2,1,0:T(8,128)} %place.1), channel_id=1, replica_groups={{0,64,128,192,256,320,384,448},{1,65,129,193,257,321,385,449},{2,66,130..., dimensions={0} | all-to-all | bytes 4718592 | tf_op jit(solution)/shard_map/all_to_all | solution.py:147
  59.9 6.0 %sum.1 = (f32[32,16,256]{2,1,0:T(8,128)}, f32[256,256]{1,0:T(8,128)}) custom-call(s32[2]{0:T(128)} %pad_add_fusion.where_ref, f32[8,2,144,256]{3,2,1,0:T(8,128)} %all_to_all.10.ids_ref.got_ref, f32[8,2,144,256]{3,2,1,0:T(8,128)} %all_to_all.10.ids_ref.got_ref), custom_call_target="tpu_custom_call" | custom-call | tf_op jit(solution)/shard_map/sum/pallas_call | solution.py:149
  65.9 9.3 %all-to-all-start.1 = ((f32[32,16,256]{2,1,0:T(8,128)}), f32[32,16,256]{2,1,0:T(8,128)S(1)}, u32[]{:S(2)}, u32[]{:S(2)}) async-start(f32[32,16,256]{2,1,0:T(8,128)} %get-tuple-element.12), calls=%async_computation.1 | async-start | bytes 1048576 | tf_op jit(solution)/shard_map/all_to_all | solution.py:178
  75.2 1.9 %gram.1 = f32[32,256]{1,0:T(8,128)} custom-call(s32[2]{0:T(128)} %pad_add_fusion.where_ref, f32[256,256]{1,0:T(8,128)} %get-tuple-element.11.factor_ref), custom_call_target="tpu_custom_call" | custom-call | tf_op jit(solution)/shard_map/gram/pallas_call | solution.py:168
  77.0 0.7 slice.9
  77.8 1.3 %collective-permute-start.1 = (f32[16,256]{1,0:T(8,128)S(1)}, f32[16,256]{1,0:T(8,128)S(1)}, u32[]{:S(2)}, u32[]{:S(2)}) collective-permute-start(f32[16,256]{1,0:T(8,128)S(1)} %slice.9), channel_id=1, source_target_pairs={{0,32},{1,33},{2,34},{3,35},{4,36},{5,37},{6,38},{7,39},{8,40},{9,... | collective-permute-start | bytes 49160 | tf_op jit(solution)/shard_map/ppermute | solution.py:176
  79.1 5.4 %all-to-all-done.1 = f32[32,16,256]{2,1,0:T(8,128)S(1)} async-done(((f32[32,16,256]{2,1,0:T(8,128)}), f32[32,16,256]{2,1,0:T(8,128)S(1)}, u32[]{:S(2)}, u32[]{:S(2)}) %all-to-all-start.1) | async-done | bytes 524320 | tf_op jit(solution)/shard_map/all_to_all | solution.py:178
  84.5 4.9 %collective-permute-start.2 = (f32[16,256]{1,0:T(8,128)S(1)}, f32[16,256]{1,0:T(8,128)S(1)}, u32[]{:S(2)}, u32[]{:S(2)}) collective-permute-start(f32[16,256]{1,0:T(8,128)S(1)} %reduce_sum.9), channel_id=1, source_target_pairs={{32,32},{33,96},{34,160},{35,224},{36,288},{37,352},{38,416},{39,4... | collective-permute-start | bytes 49160 | tf_op jit(solution)/shard_map/ppermute | solution.py:180
  89.4 0.0 collective-permute-done.1
  89.4 8.3 %collective-permute-done.2 = f32[16,256]{1,0:T(8,128)S(1)} collective-permute-done((f32[16,256]{1,0:T(8,128)S(1)}, f32[16,256]{1,0:T(8,128)S(1)}, u32[]{:S(2)}, u32[]{:S(2)}) %collective-permute-start.2) | collective-permute-done | bytes 16416 | tf_op jit(solution)/shard_map/ppermute | solution.py:180
  97.7 1.3 %fusion.1 = f32[1,16,256]{2,1,0:T(8,128)} fusion(f32[16,256]{1,0:T(8,128)S(1)} %reduce_sum.9, f32[32,256]{1,0:T(8,128)} %gram.1, f32[16,256]{1,0:T(8,128)S(1)} %collective-permute-done.1, f32[16,256]{1,0:T(8,128)S(1)} %collective-permute-done.2, pred[]{:T(512)S(6)} %eq.5), kind=kLoop, calls=%fused_computation.2 | loop fusion | flops 12288 | bytes 81921 | tf_op jit(solution)/shard_map/broadcast_in_dim | solution.py:181
  (1 shorter events, 0.0 us)
Async XLA Ops:
  9.4 5.2 %collective-permute-start = (f32[8,144,256]{2,1,0:T(8,128)}, f32[8,144,256]{2,1,0:T(8,128)S(1)}, u32[]{:S(2)}, u32[]{:S(2)}) collective-permute-start(f32[8,144,256]{2,1,0:T(8,128)} %get-tuple-element.10), channel_id=1, source_target_pairs={{0,32},{1,33},{2,34},{3,35},{4,36},{5,37},{6,38},{7,39},{8,40},{9,... | collective-permute-start | bytes 3538952 | tf_op jit(solution)/shard_map/ppermute | solution.py:136
  14.6 1.0 %copy-start = (f32[8,144,256]{2,1,0:T(8,128)}, f32[8,144,256]{2,1,0:T(8,128)S(1)}, u32[]{:S(2)}) copy-start(f32[8,144,256]{2,1,0:T(8,128)S(1)} %collective-permute-done.arrived_ref) | copy-start | bytes 3538948
  65.9 18.6 %all-to-all-start.1 = ((f32[32,16,256]{2,1,0:T(8,128)}), f32[32,16,256]{2,1,0:T(8,128)S(1)}, u32[]{:S(2)}, u32[]{:S(2)}) async-start(f32[32,16,256]{2,1,0:T(8,128)} %get-tuple-element.12), calls=%async_computation.1 | async-start | bytes 1048576 | tf_op jit(solution)/shard_map/all_to_all | solution.py:178
  77.8 11.6 %collective-permute-start.1 = (f32[16,256]{1,0:T(8,128)S(1)}, f32[16,256]{1,0:T(8,128)S(1)}, u32[]{:S(2)}, u32[]{:S(2)}) collective-permute-start(f32[16,256]{1,0:T(8,128)S(1)} %slice.9), channel_id=1, source_target_pairs={{0,32},{1,33},{2,34},{3,35},{4,36},{5,37},{6,38},{7,39},{8,40},{9,... | collective-permute-start | bytes 49160 | tf_op jit(solution)/shard_map/ppermute | solution.py:176
  84.5 13.2 %collective-permute-start.2 = (f32[16,256]{1,0:T(8,128)S(1)}, f32[16,256]{1,0:T(8,128)S(1)}, u32[]{:S(2)}, u32[]{:S(2)}) collective-permute-start(f32[16,256]{1,0:T(8,128)S(1)} %reduce_sum.9), channel_id=1, source_target_pairs={{32,32},{33,96},{34,160},{35,224},{36,288},{37,352},{38,416},{39,4... | collective-permute-start | bytes 49160 | tf_op jit(solution)/shard_map/ppermute | solution.py:180

commit v3 on v1

v3 whole, which is shorter than its diff:
```python
import jax
import jax.numpy as jnp
from jax import lax
from jax.experimental import pallas as pl
from jax.experimental.pallas import tpu as pltpu
from jax.sharding import PartitionSpec as P

NY, NC, NX, NZ = 8, 2, 4, 8
BOTH = ("row", "col")


def flat(y, c, x, z):
    return ((y * NC + c) * NX + x) * NZ + z


def every():
    return [(y, c, x, z) for y in range(NY) for c in range(NC) for x in range(NX) for z in range(NZ)]


LINES = [[flat(y, 0, x, z) for y in range(NY)] for x in range(NX) for z in range(NZ)] + [
    [flat(y, 1, x, z) for z in range(NZ)] for x in range(NX) for y in range(NY)
]
PLANES = [[flat(y, 0, x, z) for x in range(NX) for z in range(NZ)] for y in range(NY)] + [
    [flat(y, 1, x, z) for x in range(NX) for y in range(NY)] for z in range(NZ)
]
PARTNER = [(flat(y, c, x, z), flat(y, 1 - c, x, z)) for y, c, x, z in every()]
TO_ODD = [(flat(y, 0, x, z), flat(y, 1, x, z)) for y, c, x, z in every() if c == 0]
TURN = [(flat(y, 1, x, z), flat(z, 1, x, y)) for y, c, x, z in every() if c == 1]


def split(a):
    high = a.astype(jnp.bfloat16)
    return high, (a - high.astype(jnp.float32)).astype(jnp.bfloat16)


def times(turned, b):
    ah, al = split(turned)
    bh, bl = split(b)
    left = jnp.concatenate([ah, ah, al], axis=1)
    right = jnp.concatenate([bh, bl, bh], axis=0)
    return jnp.dot(left, right, preferred_element_type=jnp.float32)


def tile_of(ids_ref, rows_ref, index):
    share, width = rows_ref.shape[1:]
    first = share * index + 1
    row = lax.broadcasted_iota(jnp.int32, (share, width), 0)
    lane = lax.broadcasted_iota(jnp.int32, (share, width), 1)
    tile = jnp.where(lane < first + row, rows_ref[0], 0.0)
    for s in range(ids_ref.shape[0]):
        tile = jnp.where((row == 0) & (lane == first + s), ids_ref[s].astype(jnp.float32), tile)
    return tile


def sent_kernel(ids_ref, left_ref, right_ref, rows_ref, sent_ref, own_ref, held_ref, tile_ref, scratch_ref, sems):
    slots = left_ref.shape[0]
    share, width = rows_ref.shape[1:]
    copies = []
    for s in range(slots):
        pair = (
            pltpu.make_async_copy(left_ref.at[s], scratch_ref.at[s], sems.at[0, s]),
            pltpu.make_async_copy(right_ref.at[s], held_ref.at[s], sems.at[1, s]),
        )
        for copy in pair:
            copy.start()
        copies.append(pair)
    index = lax.axis_index("row")
    core = index % NC
    tile = tile_of(ids_ref, rows_ref, index)
    tile_ref[...] = tile
    for d in range(NY):
        sent_ref[d, slots * share :] = tile
    for s in range(slots):
        for copy in copies[s]:
            copy.wait()
        turned = scratch_ref[s].T.reshape(NY, NC, share, width)
        even, odd = turned[:, 0].reshape(NY * share, width), turned[:, 1].reshape(NY * share, width)
        own_ref[s] = jnp.where(core == 0, even, odd)
        product = times(jnp.where(core == 0, odd, even), held_ref[s])
        sent_ref[:, s * share : (s + 1) * share] = product.reshape(NY, share, width)


def kept_kernel(own_ref, held_ref, tile_ref, kept_ref):
    slots = own_ref.shape[0]
    share, width = tile_ref.shape
    for s in range(slots):
        product = times(own_ref[s], held_ref[s])
        kept_ref[:, s * share : (s + 1) * share] = product.reshape(NY, share, width)
    for d in range(NY):
        kept_ref[d, slots * share :] = tile_ref[...]


def place_kernel(kept_ref, arrived_ref, out_ref):
    for d in range(NY):
        out_ref[d, 0] = kept_ref[d]
        out_ref[d, 1] = arrived_ref[d]


def sum_kernel(got_ref, out_ref, factor_ref, ids_ref, sem):
    share = out_ref.shape[1]
    slots = got_ref.shape[2] // share - 1
    base = slots * share
    copy = pltpu.make_async_copy(got_ref.at[:, :, base : base + 8], ids_ref, sem)
    copy.start()
    index = lax.axis_index("row")
    core = index % NC
    out_ref[...] = jnp.zeros_like(out_ref)

    def first_of(m, half):
        source_core = core if half == 0 else 1 - core
        return share * (jnp.where(core == 0, m, index // NC) * NC + source_core) + 1

    for m in range(NY):
        for half in range(NC):
            tile = got_ref[m, half, base:]
            row = lax.broadcasted_iota(jnp.int32, tile.shape, 0)
            lane = lax.broadcasted_iota(jnp.int32, tile.shape, 1)
            at = (m * NC + half) * share
            factor_ref[at : at + share] = jnp.where(lane < first_of(m, half) + row, tile, 0.0)
    copy.wait()

    def member(m, carry):
        for half in range(NC):
            first = first_of(m, half)
            for s in range(slots):
                k = ids_ref[m, half, 0, first + s].astype(jnp.int32)
                out_ref[k] += got_ref[m, half, s * share : (s + 1) * share]
        return carry

    lax.fori_loop(0, NY, member, 0)


def gram_kernel(factor_ref, own_ref, other_ref, whole_ref):
    whole_ref[...] = times(factor_ref[...].T, factor_ref[...])
    share = own_ref.shape[0]
    start = lax.axis_index("row") // NC * (NC * share)
    own_ref[...] = whole_ref[pl.ds(pl.multiple_of(start, share), share)]
    other_ref[...] = whole_ref[pl.ds(pl.multiple_of(start + share, share), share)]


def on_device(lhat, ainv_anc, diag_inv, targets):
    slots, height, width = lhat.shape
    core = lax.axis_index("row") % NC
    share = diag_inv.shape[1]
    supers = NX * NZ
    length = (slots + 1) * share
    smem, vmem, hbm = (pl.BlockSpec(memory_space=m) for m in (pltpu.SMEM, pltpu.VMEM, pltpu.HBM))

    def here(*lengths):
        return pltpu.VMEM(lengths, jnp.float32)

    def on_chip(x):
        return pltpu.with_memory_space_constraint(x, pltpu.VMEM)

    def call(kernel, ins, outs, mib, *args, scratch=()):
        return pl.pallas_call(
            kernel,
            in_specs=ins,
            out_specs=[vmem] * len(outs),
            out_shape=outs,
            scratch_shapes=scratch,
            compiler_params=pltpu.CompilerParams(vmem_limit_bytes=mib << 20),
            name=kernel.__name__,
        )(*args)

    sent, own, held, tile = call(
        sent_kernel,
        [smem, hbm, hbm, vmem],
        [here(NY, length, width), here(slots, NY * share, width), here(slots, height, width), here(share, width)],
        24,
        targets.reshape(slots),
        pltpu.with_memory_space_constraint(lhat, pltpu.HBM),
        pltpu.with_memory_space_constraint(ainv_anc, pltpu.HBM),
        diag_inv,
        scratch=[pltpu.VMEM((slots, height, width), jnp.float32), pltpu.SemaphoreType.DMA((2, slots))],
    )
    arrived = lax.ppermute(sent, BOTH, PARTNER)
    (kept,) = call(kept_kernel, [vmem] * 3, [here(NY, length, width)], 24, on_chip(own), on_chip(held), on_chip(tile))
    (payload,) = call(place_kernel, [vmem] * 2, [here(NY, NC, length, width)], 24, on_chip(kept), on_chip(arrived))

    got = lax.all_to_all(payload, BOTH, 0, 0, axis_index_groups=LINES, tiled=True)

    summed, factor = call(
        sum_kernel,
        [vmem],
        [here(supers, share, width), here(NY * NC * share, width)],
        24,
        on_chip(got),
        scratch=[pltpu.SMEM((NY, NC, 8, width), jnp.float32), pltpu.SemaphoreType.DMA],
    )

    gram, gram_other = call(
        gram_kernel, [vmem], [here(share, width), here(share, width)], 24, on_chip(factor),
        scratch=[pltpu.VMEM((width, width), jnp.float32)],
    )
    gram_odd = lax.ppermute(gram_other, BOTH, TO_ODD)

    parts = lax.all_to_all(summed, BOTH, 0, 0, axis_index_groups=PLANES, tiled=True)
    total = jnp.sum(parts, axis=0)
    turned = lax.ppermute(total, BOTH, TURN)
    return jnp.where(core == 0, gram - total, gram_odd - turned)[None]


def solution(mesh):
    placed = (
        P(("row", "col"), None, None),
        P(("row", "col"), None, None),
        P("col", "row", None),
        P(("row", "col"), None),
    )
    return jax.shard_map(
        on_device, mesh=mesh, in_specs=placed, out_specs=P("col", "row", None), check_vma=False
    )
```

time: 98 us -> 89.6 us (0.914)
  blocking collectives: 0 us -> 41.6 us
  waiting for transfers between devices: 48.5 us -> 17.7 us
  starting transfers between devices: 29.9 us -> 18 us
  Pallas kernels: 0 us -> 9.64 us
  local copies, waits for them, and re-layouts: 9.23 us -> 1.37 us
  matrix products: 5.93 us -> 0 us
  other arithmetic: 3.69 us -> 0.66 us
    all_to_all x0 -> x1, blocking collectives: none -> 41.6 us  [on_device(): lax.all_to_all(payload, BOTH, 0, 0, axis_index_groups=LINES, tiled=True)]
    all_to_all x1 -> x0, waiting for transfers between devices: 33.4 us -> none  [on_device(): lax.all_to_all(payload, BOTH, 0, 0, axis_index_groups=LINES, tiled=True)]
    all_to_all x1 -> x0, starting transfers between devices: 10 us -> none  [on_device(): lax.all_to_all(payload, BOTH, 0, 0, axis_index_groups=LINES, tiled=True)]
    pallas_call x0 -> x5, Pallas kernels: none -> 9.64 us  [call(): pl.pallas_call(kernel, in_specs=ins, out_specs=[vmem] * len(outs), out_sh...]
    dot_general x4 -> x0, matrix products: 5.93 us -> none  [the longest x2 4.06 us: product(): jnp.einsum('shdr,shj->dsrj', left, ainv_anc, precision=lax.Precision.HIGH)]
    slice x6 -> x0, local copies, waits for them, and re-layouts: 3.5 us -> none  [the longest x1 1.73 us: on_device(): blocks = got[:, :n * share].reshape(NY * n, share, width)]
    ppermute x3 -> x2, starting transfers between devices: 7.97 us -> 6.15 us  [the longest x1 4.86 us: on_device(): turned = lax.ppermute(total, BOTH, TURN)]
    ppermute x1, waiting for transfers between devices: 0.01 us -> 1.75 us  [on_device(): arrived = lax.ppermute(sent, BOTH, PARTNER)]
  transfers between devices with their start and end apart: 6 -> 4, of which waited for: 3 -> 3; matrix products, arithmetic and copies ran while one was open for 5% -> 0% of each run, Pallas kernels for 0% -> 1%
where the time goes in v3:
time: 89.6 us; the launch traced here: 89.1 us
  blocking collectives  41.6 us (46%)
  starting transfers between devices  18 us (20%)
  waiting for transfers between devices  17.7 us (20%)
  Pallas kernels  9.64 us (11%)
  local copies, waits for them, and re-layouts  1.37 us (2%)
    all_to_all x1, blocking collectives, on_device(): lax.all_to_all(payload, BOTH, 0, 0, axis_index_groups=LINES, tiled=True)  41.6 us
    pallas_call x5, Pallas kernels, call(): pl.pallas_call(kernel, in_specs=ins, out_specs=[vmem] * len(outs), out_sh...  9.64 us
    all_to_all x1, starting transfers between devices, on_device(): lax.all_to_all(summed, BOTH, 0, 0, axis_index_groups=PLANES, tiled=True)  9.28 us
    ppermute x1, waiting for transfers between devices, on_device(): turned = lax.ppermute(total, BOTH, TURN)  8.31 us
    all_to_all x1, waiting for transfers between devices, on_device(): lax.all_to_all(summed, BOTH, 0, 0, axis_index_groups=PLANES, tiled=True)  7.68 us
    ppermute x1, starting transfers between devices, on_device(): turned = lax.ppermute(total, BOTH, TURN)  4.86 us
    ppermute x1, starting transfers between devices, on_device(): arrived = lax.ppermute(sent, BOTH, PARTNER)  2.58 us
  transfers between devices with their start and end apart: 4, of which 3 were waited for; matrix products, arithmetic and copies ran while one was open for 0% of the time, Pallas kernels for 1%

profile of v3, /device:TPU:33, one launch (start us, length us, event | category | flops | bytes accessed | tf_op | source)
XLA Modules:
  0.0 89.1 jit_solution(10953811448108838672)
XLA Ops:
  0.0 0.0 copy-start
  0.0 0.7 copy-done
  0.7 0.0 copy-start.1
  0.7 0.7 copy-done.1
  1.4 4.3 %sent_kernel.1 = (f32[8,144,256]{2,1,0:T(8,128)S(1)}, f32[8,128,256]{2,1,0:T(8,128)S(1)}, f32[8,256,256]{2,1,0:T(8,128)S(1)}, f32[16,256]{1,0:T(8,128)S(1)}) custom-call(s32[8]{0:T(128)S(1)} %bitcast.3, f32[8,256,256]{2,1,0:T(8,128)} %left_ref.1, f32[8,256,256]{2,1,0:T(8,128)} %right_ref.1, f32[1,16,256]{2,1,0:T(8,128)S(1)} %copy-done), custom_call_target="tpu_custom_call" | custom-call | tf_op jit(solution)/shard_map/sent_kernel/pallas_call | solution.py:156
  5.7 2.6 %collective-permute-start = (f32[8,144,256]{2,1,0:T(8,128)S(1)}, f32[8,144,256]{2,1,0:T(8,128)S(1)}, u32[]{:S(2)}, u32[]{:S(2)}) collective-permute-start(f32[8,144,256]{2,1,0:T(8,128)S(1)} %get-tuple-element.16), channel_id=1, source_target_pairs={{0,32},{1,33},{2,34},{3,35},{4,36},{5,37},{6,38},{7,39},{8,40},{9,... | collective-permute-start | bytes 3538952 | tf_op jit(solution)/shard_map/ppermute | solution.py:177
  8.2 0.7 kept_kernel.1.kept_ref
  8.9 1.8 %collective-permute-done.arrived_ref = f32[8,144,256]{2,1,0:T(8,128)S(1)} collective-permute-done((f32[8,144,256]{2,1,0:T(8,128)S(1)}, f32[8,144,256]{2,1,0:T(8,128)S(1)}, u32[]{:S(2)}, u32[]{:S(2)}) %collective-permute-start) | collective-permute-done | bytes 1179680 | tf_op jit(solution)/shard_map/ppermute | solution.py:177
  10.7 0.2 place_kernel.1
  10.9 41.6 %all_to_all.10.got_ref = f32[8,2,144,256]{3,2,1,0:T(8,128)S(1)} all-to-all(f32[8,2,144,256]{3,2,1,0:T(8,128)S(1)} %place_kernel.1), channel_id=1, replica_groups={{0,64,128,192,256,320,384,448},{1,65,129,193,257,321,385,449},{2,66,130..., dimensions={0} | all-to-all | bytes 4718592 | tf_op jit(solution)/shard_map/all_to_all | solution.py:181
  52.5 4.2 %sum_kernel.1 = (f32[32,16,256]{2,1,0:T(8,128)}, f32[256,256]{1,0:T(8,128)S(1)}) custom-call(f32[8,2,144,256]{3,2,1,0:T(8,128)S(1)} %all_to_all.10.got_ref), custom_call_target="tpu_custom_call" | custom-call | tf_op jit(solution)/shard_map/sum_kernel/pallas_call | solution.py:156
  56.7 9.3 %all-to-all-start.1 = ((f32[32,16,256]{2,1,0:T(8,128)}), f32[32,16,256]{2,1,0:T(8,128)S(1)}, u32[]{:S(2)}, u32[]{:S(2)}) async-start(f32[32,16,256]{2,1,0:T(8,128)} %get-tuple-element.19), calls=%async_computation.1 | async-start | bytes 1048576 | tf_op jit(solution)/shard_map/all_to_all | solution.py:198
  66.0 0.3 gram_kernel.1
  66.3 1.3 %collective-permute-start.1 = (f32[16,256]{1,0:T(8,128)S(1)}, f32[16,256]{1,0:T(8,128)S(1)}, u32[]{:S(2)}, u32[]{:S(2)}) collective-permute-start(f32[16,256]{1,0:T(8,128)S(1)} %get-tuple-element.20), channel_id=1, source_target_pairs={{0,32},{1,33},{2,34},{3,35},{4,36},{5,37},{6,38},{7,39},{8,40},{9,... | collective-permute-start | bytes 49160 | tf_op jit(solution)/shard_map/ppermute | solution.py:196
  67.6 7.7 %all-to-all-done.1 = f32[32,16,256]{2,1,0:T(8,128)S(1)} async-done(((f32[32,16,256]{2,1,0:T(8,128)}), f32[32,16,256]{2,1,0:T(8,128)S(1)}, u32[]{:S(2)}, u32[]{:S(2)}) %all-to-all-start.1) | async-done | bytes 524320 | tf_op jit(solution)/shard_map/all_to_all | solution.py:198
  75.3 4.9 %collective-permute-start.2 = (f32[16,256]{1,0:T(8,128)S(1)}, f32[16,256]{1,0:T(8,128)S(1)}, u32[]{:S(2)}, u32[]{:S(2)}) collective-permute-start(f32[16,256]{1,0:T(8,128)S(1)} %reduce_sum.9), channel_id=1, source_target_pairs={{32,32},{33,96},{34,160},{35,224},{36,288},{37,352},{38,416},{39,4... | collective-permute-start | bytes 49160 | tf_op jit(solution)/shard_map/ppermute | solution.py:200
  80.2 0.0 collective-permute-done.1
  80.2 8.3 %collective-permute-done.2 = f32[16,256]{1,0:T(8,128)S(1)} collective-permute-done((f32[16,256]{1,0:T(8,128)S(1)}, f32[16,256]{1,0:T(8,128)S(1)}, u32[]{:S(2)}, u32[]{:S(2)}) %collective-permute-start.2) | collective-permute-done | bytes 16416 | tf_op jit(solution)/shard_map/ppermute | solution.py:200
  88.5 0.6 select_bitcast_fusion
  (1 shorter events, 0.0 us)
Async XLA Ops:
  0.0 0.7 copy-start
  0.7 0.7 copy-start.1
  5.7 5.0 %collective-permute-start = (f32[8,144,256]{2,1,0:T(8,128)S(1)}, f32[8,144,256]{2,1,0:T(8,128)S(1)}, u32[]{:S(2)}, u32[]{:S(2)}) collective-permute-start(f32[8,144,256]{2,1,0:T(8,128)S(1)} %get-tuple-element.16), channel_id=1, source_target_pairs={{0,32},{1,33},{2,34},{3,35},{4,36},{5,37},{6,38},{7,39},{8,40},{9,... | collective-permute-start | bytes 3538952 | tf_op jit(solution)/shard_map/ppermute | solution.py:177
  56.7 18.6 %all-to-all-start.1 = ((f32[32,16,256]{2,1,0:T(8,128)}), f32[32,16,256]{2,1,0:T(8,128)S(1)}, u32[]{:S(2)}, u32[]{:S(2)}) async-start(f32[32,16,256]{2,1,0:T(8,128)} %get-tuple-element.19), calls=%async_computation.1 | async-start | bytes 1048576 | tf_op jit(solution)/shard_map/all_to_all | solution.py:198
  66.3 13.9 %collective-permute-start.1 = (f32[16,256]{1,0:T(8,128)S(1)}, f32[16,256]{1,0:T(8,128)S(1)}, u32[]{:S(2)}, u32[]{:S(2)}) collective-permute-start(f32[16,256]{1,0:T(8,128)S(1)} %get-tuple-element.20), channel_id=1, source_target_pairs={{0,32},{1,33},{2,34},{3,35},{4,36},{5,37},{6,38},{7,39},{8,40},{9,... | collective-permute-start | bytes 49160 | tf_op jit(solution)/shard_map/ppermute | solution.py:196
  75.3 13.2 %collective-permute-start.2 = (f32[16,256]{1,0:T(8,128)S(1)}, f32[16,256]{1,0:T(8,128)S(1)}, u32[]{:S(2)}, u32[]{:S(2)}) collective-permute-start(f32[16,256]{1,0:T(8,128)S(1)} %reduce_sum.9), channel_id=1, source_target_pairs={{32,32},{33,96},{34,160},{35,224},{36,288},{37,352},{38,416},{39,4... | collective-permute-start | bytes 49160 | tf_op jit(solution)/shard_map/ppermute | solution.py:200

commit v4 on v3

--- a/solution.py
+++ b/solution.py
@@ -25,7 +25,8 @@
 ]
 PARTNER = [(flat(y, c, x, z), flat(y, 1 - c, x, z)) for y, c, x, z in every()]
 TO_ODD = [(flat(y, 0, x, z), flat(y, 1, x, z)) for y, c, x, z in every() if c == 0]
-TURN = [(flat(y, 1, x, z), flat(z, 1, x, y)) for y, c, x, z in every() if c == 1]
+FAR = NY // 2
+TURN = [(flat(y, 1, x, z), flat(z, 1, x, (y + FAR) % NZ)) for y, c, x, z in every() if c == 1]
 
 
 def split(a):
@@ -52,9 +53,17 @@
     return tile
 
 
-def sent_kernel(ids_ref, left_ref, right_ref, rows_ref, sent_ref, own_ref, held_ref, tile_ref, scratch_ref, sems):
+def sent_kernel(
+    ids_hbm, left_ref, right_ref, rows_hbm, sent_ref, own_ref, held_ref, tile_ref, ids_ref, rows_ref, scratch_ref, small, sems
+):
     slots = left_ref.shape[0]
     share, width = rows_ref.shape[1:]
+    few = (
+        pltpu.make_async_copy(ids_hbm, ids_ref, small.at[0]),
+        pltpu.make_async_copy(rows_hbm, rows_ref, small.at[1]),
+    )
+    for copy in few:
+        copy.start()
     copies = []
     for s in range(slots):
         pair = (
@@ -66,6 +75,8 @@
         copies.append(pair)
     index = lax.axis_index("row")
     core = index % NC
+    for copy in few:
+        copy.wait()
     tile = tile_of(ids_ref, rows_ref, index)
     tile_ref[...] = tile
     for d in range(NY):
@@ -100,10 +111,11 @@
     share = out_ref.shape[1]
     slots = got_ref.shape[2] // share - 1
     base = slots * share
-    copy = pltpu.make_async_copy(got_ref.at[:, :, base : base + 8], ids_ref, sem)
+    copy = pltpu.make_async_copy(got_ref.at[:, :, base : base + 1], ids_ref, sem)
     copy.start()
     index = lax.axis_index("row")
     core = index % NC
+    flip = core * FAR
     out_ref[...] = jnp.zeros_like(out_ref)
 
     def first_of(m, half):
@@ -124,7 +136,7 @@
             first = first_of(m, half)
             for s in range(slots):
                 k = ids_ref[m, half, 0, first + s].astype(jnp.int32)
-                out_ref[k] += got_ref[m, half, s * share : (s + 1) * share]
+                out_ref[k ^ flip] += got_ref[m, half, s * share : (s + 1) * share]
         return carry
 
     lax.fori_loop(0, NY, member, 0)
@@ -144,7 +156,7 @@
     share = diag_inv.shape[1]
     supers = NX * NZ
     length = (slots + 1) * share
-    smem, vmem, hbm = (pl.BlockSpec(memory_space=m) for m in (pltpu.SMEM, pltpu.VMEM, pltpu.HBM))
+    vmem, hbm = (pl.BlockSpec(memory_space=m) for m in (pltpu.VMEM, pltpu.HBM))
 
     def here(*lengths):
         return pltpu.VMEM(lengths, jnp.float32)
@@ -165,14 +177,20 @@
 
     sent, own, held, tile = call(
         sent_kernel,
-        [smem, hbm, hbm, vmem],
+        [hbm] * 4,
         [here(NY, length, width), here(slots, NY * share, width), here(slots, height, width), here(share, width)],
         24,
-        targets.reshape(slots),
-        pltpu.with_memory_space_constraint(lhat, pltpu.HBM),
-        pltpu.with_memory_space_constraint(ainv_anc, pltpu.HBM),
-        diag_inv,
-        scratch=[pltpu.VMEM((slots, height, width), jnp.float32), pltpu.SemaphoreType.DMA((2, slots))],
+        *(
+            pltpu.with_memory_space_constraint(x, pltpu.HBM)
+            for x in (targets.reshape(slots), lhat, ainv_anc, diag_inv)
+        ),
+        scratch=[
+            pltpu.SMEM((slots,), jnp.int32),
+            pltpu.VMEM((1, share, width), jnp.float32),
+            pltpu.VMEM((slots, height, width), jnp.float32),
+            pltpu.SemaphoreType.DMA((2,)),
+            pltpu.SemaphoreType.DMA((2, slots)),
+        ],
     )
     arrived = lax.ppermute(sent, BOTH, PARTNER)
     (kept,) = call(kept_kernel, [vmem] * 3, [here(NY, length, width)], 24, on_chip(own), on_chip(held), on_chip(tile))
@@ -186,7 +204,7 @@
         [here(supers, share, width), here(NY * NC * share, width)],
         24,
         on_chip(got),
-        scratch=[pltpu.SMEM((NY, NC, 8, width), jnp.float32), pltpu.SemaphoreType.DMA],
+        scratch=[pltpu.SMEM((NY, NC, 1, width), jnp.float32), pltpu.SemaphoreType.DMA],
     )
 
     gram, gram_other = call(

time: 89.6 us -> 85.8 us (0.958)
  the two profiles are of different devices: /device:TPU:33 before, /device:TPU:9 now
where the time goes in v4:
time: 85.8 us; the launch traced here: 85.5 us
  blocking collectives  41.6 us (48%)
  waiting for transfers between devices  19.4 us (23%)
  starting transfers between devices  15.4 us (18%)
  Pallas kernels  8.36 us (10%)
    all_to_all x1, blocking collectives, on_device(): lax.all_to_all(payload, BOTH, 0, 0, axis_index_groups=LINES, tiled=True)  41.6 us
    all_to_all x1, waiting for transfers between devices, on_device(): lax.all_to_all(summed, BOTH, 0, 0, axis_index_groups=PLANES, tiled=True)  11.1 us
    all_to_all x1, starting transfers between devices, on_device(): lax.all_to_all(summed, BOTH, 0, 0, axis_index_groups=PLANES, tiled=True)  9.62 us
    pallas_call x5, Pallas kernels, call(): pl.pallas_call(kernel, in_specs=ins, out_specs=[vmem] * len(outs), out_sh...  8.36 us
    ppermute x1, waiting for transfers between devices, on_device(): turned = lax.ppermute(total, BOTH, TURN)  6.45 us
    ppermute x1, starting transfers between devices, on_device(): arrived = lax.ppermute(sent, BOTH, PARTNER)  2.58 us
    ppermute x1, starting transfers between devices, on_device(): turned = lax.ppermute(total, BOTH, TURN)  1.92 us
    ppermute x1, waiting for transfers between devices, on_device(): arrived = lax.ppermute(sent, BOTH, PARTNER)  1.75 us
  transfers between devices with their start and end apart: 4, of which 3 were waited for; matrix products, arithmetic and copies ran while one was open for 0% of the time, Pallas kernels for 1%

profile of v4, /device:TPU:9, one launch (start us, length us, event | category | flops | bytes accessed | tf_op | source)
XLA Modules:
  0.0 85.5 jit_solution(14350512771342095852)
XLA Ops:
  0.0 4.9 %sent_kernel.1 = (f32[8,144,256]{2,1,0:T(8,128)S(1)}, f32[8,128,256]{2,1,0:T(8,128)S(1)}, f32[8,256,256]{2,1,0:T(8,128)S(1)}, f32[16,256]{1,0:T(8,128)S(1)}) custom-call(s32[8]{0:T(128)} %bitcast.3, f32[8,256,256]{2,1,0:T(8,128)} %left_ref.1, f32[8,256,256]{2,1,0:T(8,128)} %right_ref.1, f32[1,16,256]{2,1,0:T(8,128)} %rows_hbm.1), custom_call_target="tpu_custom_call" | custom-call | tf_op jit(solution)/shard_map/sent_kernel/pallas_call | solution.py:168
  4.9 2.6 %collective-permute-start = (f32[8,144,256]{2,1,0:T(8,128)S(1)}, f32[8,144,256]{2,1,0:T(8,128)S(1)}, u32[]{:S(2)}, u32[]{:S(2)}) collective-permute-start(f32[8,144,256]{2,1,0:T(8,128)S(1)} %get-tuple-element.16), channel_id=1, source_target_pairs={{0,32},{1,33},{2,34},{3,35},{4,36},{5,37},{6,38},{7,39},{8,40},{9,... | collective-permute-start | bytes 3538952 | tf_op jit(solution)/shard_map/ppermute | solution.py:195
  7.5 0.7 kept_kernel.1.kept_ref
  8.2 1.8 %collective-permute-done.arrived_ref = f32[8,144,256]{2,1,0:T(8,128)S(1)} collective-permute-done((f32[8,144,256]{2,1,0:T(8,128)S(1)}, f32[8,144,256]{2,1,0:T(8,128)S(1)}, u32[]{:S(2)}, u32[]{:S(2)}) %collective-permute-start) | collective-permute-done | bytes 1179680 | tf_op jit(solution)/shard_map/ppermute | solution.py:195
  9.9 0.2 place_kernel.1
  10.1 41.6 %all_to_all.10.got_ref = f32[8,2,144,256]{3,2,1,0:T(8,128)S(1)} all-to-all(f32[8,2,144,256]{3,2,1,0:T(8,128)S(1)} %place_kernel.1), channel_id=1, replica_groups={{0,64,128,192,256,320,384,448},{1,65,129,193,257,321,385,449},{2,66,130..., dimensions={0} | all-to-all | bytes 4718592 | tf_op jit(solution)/shard_map/all_to_all | solution.py:199
  51.7 2.3 %sum_kernel.1 = (f32[32,16,256]{2,1,0:T(8,128)}, f32[256,256]{1,0:T(8,128)S(1)}) custom-call(f32[8,2,144,256]{3,2,1,0:T(8,128)S(1)} %all_to_all.10.got_ref), custom_call_target="tpu_custom_call" | custom-call | tf_op jit(solution)/shard_map/sum_kernel/pallas_call | solution.py:168
  54.1 9.6 %all-to-all-start.1 = ((f32[32,16,256]{2,1,0:T(8,128)}), f32[32,16,256]{2,1,0:T(8,128)S(1)}, u32[]{:S(2)}, u32[]{:S(2)}) async-start(f32[32,16,256]{2,1,0:T(8,128)} %get-tuple-element.19), calls=%async_computation.1 | async-start | bytes 1048576 | tf_op jit(solution)/shard_map/all_to_all | solution.py:216
  63.7 0.3 gram_kernel.1
  64.0 1.3 %collective-permute-start.1 = (f32[16,256]{1,0:T(8,128)S(1)}, f32[16,256]{1,0:T(8,128)S(1)}, u32[]{:S(2)}, u32[]{:S(2)}) collective-permute-start(f32[16,256]{1,0:T(8,128)S(1)} %get-tuple-element.20), channel_id=1, source_target_pairs={{0,32},{1,33},{2,34},{3,35},{4,36},{5,37},{6,38},{7,39},{8,40},{9,... | collective-permute-start | bytes 49160 | tf_op jit(solution)/shard_map/ppermute | solution.py:214
  65.3 11.1 %all-to-all-done.1 = f32[32,16,256]{2,1,0:T(8,128)S(1)} async-done(((f32[32,16,256]{2,1,0:T(8,128)}), f32[32,16,256]{2,1,0:T(8,128)S(1)}, u32[]{:S(2)}, u32[]{:S(2)}) %all-to-all-start.1) | async-done | bytes 524320 | tf_op jit(solution)/shard_map/all_to_all | solution.py:216
  76.5 1.9 %collective-permute-start.2 = (f32[16,256]{1,0:T(8,128)S(1)}, f32[16,256]{1,0:T(8,128)S(1)}, u32[]{:S(2)}, u32[]{:S(2)}) collective-permute-start(f32[16,256]{1,0:T(8,128)S(1)} %reduce_sum.9), channel_id=1, source_target_pairs={{32,36},{33,100},{34,164},{35,228},{36,292},{37,356},{38,420},{39,... | collective-permute-start | bytes 49160 | tf_op jit(solution)/shard_map/ppermute | solution.py:218
  78.4 0.0 collective-permute-done.1
  78.4 6.5 %collective-permute-done.2 = f32[16,256]{1,0:T(8,128)S(1)} collective-permute-done((f32[16,256]{1,0:T(8,128)S(1)}, f32[16,256]{1,0:T(8,128)S(1)}, u32[]{:S(2)}, u32[]{:S(2)}) %collective-permute-start.2) | collective-permute-done | bytes 16416 | tf_op jit(solution)/shard_map/ppermute | solution.py:218
  84.9 0.6 select_bitcast_fusion
  (1 shorter events, 0.0 us)
Async XLA Ops:
  4.9 5.0 %collective-permute-start = (f32[8,144,256]{2,1,0:T(8,128)S(1)}, f32[8,144,256]{2,1,0:T(8,128)S(1)}, u32[]{:S(2)}, u32[]{:S(2)}) collective-permute-start(f32[8,144,256]{2,1,0:T(8,128)S(1)} %get-tuple-element.16), channel_id=1, source_target_pairs={{0,32},{1,33},{2,34},{3,35},{4,36},{5,37},{6,38},{7,39},{8,40},{9,... | collective-permute-start | bytes 3538952 | tf_op jit(solution)/shard_map/ppermute | solution.py:195
  54.1 22.4 %all-to-all-start.1 = ((f32[32,16,256]{2,1,0:T(8,128)}), f32[32,16,256]{2,1,0:T(8,128)S(1)}, u32[]{:S(2)}, u32[]{:S(2)}) async-start(f32[32,16,256]{2,1,0:T(8,128)} %get-tuple-element.19), calls=%async_computation.1 | async-start | bytes 1048576 | tf_op jit(solution)/shard_map/all_to_all | solution.py:216
  64.0 14.4 %collective-permute-start.1 = (f32[16,256]{1,0:T(8,128)S(1)}, f32[16,256]{1,0:T(8,128)S(1)}, u32[]{:S(2)}, u32[]{:S(2)}) collective-permute-start(f32[16,256]{1,0:T(8,128)S(1)} %get-tuple-element.20), channel_id=1, source_target_pairs={{0,32},{1,33},{2,34},{3,35},{4,36},{5,37},{6,38},{7,39},{8,40},{9,... | collective-permute-start | bytes 49160 | tf_op jit(solution)/shard_map/ppermute | solution.py:214
  76.5 8.4 %collective-permute-start.2 = (f32[16,256]{1,0:T(8,128)S(1)}, f32[16,256]{1,0:T(8,128)S(1)}, u32[]{:S(2)}, u32[]{:S(2)}) collective-permute-start(f32[16,256]{1,0:T(8,128)S(1)} %reduce_sum.9), channel_id=1, source_target_pairs={{32,36},{33,100},{34,164},{35,228},{36,292},{37,356},{38,420},{39,... | collective-permute-start | bytes 49160 | tf_op jit(solution)/shard_map/ppermute | solution.py:218

commit v5 on v4

--- a/solution.py
+++ b/solution.py
@@ -4,6 +4,7 @@
 from jax.experimental import pallas as pl
 from jax.experimental.pallas import tpu as pltpu
 from jax.sharding import PartitionSpec as P
+
 
 NY, NC, NX, NZ = 8, 2, 4, 8
 BOTH = ("row", "col")
@@ -35,7 +36,7 @@
 
 
 def times(turned, b):
-    ah, al = split(turned)
+    ah, al = turned
     bh, bl = split(b)
     left = jnp.concatenate([ah, ah, al], axis=1)
     right = jnp.concatenate([bh, bl, bh], axis=0)
@@ -75,27 +76,30 @@
         copies.append(pair)
     index = lax.axis_index("row")
     core = index % NC
+    for s in range(slots):
+        for copy in copies[s]:
+            copy.wait()
+        parts = []
+        for i, part in enumerate(split(scratch_ref[s])):
+            part = part.T.reshape(NY, NC, share, width)
+            even, odd = part[:, 0].reshape(NY * share, width), part[:, 1].reshape(NY * share, width)
+            own_ref[i, s] = jnp.where(core == 0, even, odd)
+            parts.append(jnp.where(core == 0, odd, even))
+        product = times(parts, held_ref[s])
+        sent_ref[:, s * share : (s + 1) * share] = product.reshape(NY, share, width)
     for copy in few:
         copy.wait()
     tile = tile_of(ids_ref, rows_ref, index)
     tile_ref[...] = tile
     for d in range(NY):
         sent_ref[d, slots * share :] = tile
-    for s in range(slots):
-        for copy in copies[s]:
-            copy.wait()
-        turned = scratch_ref[s].T.reshape(NY, NC, share, width)
-        even, odd = turned[:, 0].reshape(NY * share, width), turned[:, 1].reshape(NY * share, width)
-        own_ref[s] = jnp.where(core == 0, even, odd)
-        product = times(jnp.where(core == 0, odd, even), held_ref[s])
-        sent_ref[:, s * share : (s + 1) * share] = product.reshape(NY, share, width)
 
 
 def kept_kernel(own_ref, held_ref, tile_ref, kept_ref):
-    slots = own_ref.shape[0]
+    slots = held_ref.shape[0]
     share, width = tile_ref.shape
     for s in range(slots):
-        product = times(own_ref[s], held_ref[s])
+        product = times((own_ref[0, s], own_ref[1, s]), held_ref[s])
         kept_ref[:, s * share : (s + 1) * share] = product.reshape(NY, share, width)
     for d in range(NY):
         kept_ref[d, slots * share :] = tile_ref[...]
@@ -143,7 +147,7 @@
 
 
 def gram_kernel(factor_ref, own_ref, other_ref, whole_ref):
-    whole_ref[...] = times(factor_ref[...].T, factor_ref[...])
+    whole_ref[...] = times(split(factor_ref[...].T), factor_ref[...])
     share = own_ref.shape[0]
     start = lax.axis_index("row") // NC * (NC * share)
     own_ref[...] = whole_ref[pl.ds(pl.multiple_of(start, share), share)]
@@ -158,8 +162,8 @@
     length = (slots + 1) * share
     vmem, hbm = (pl.BlockSpec(memory_space=m) for m in (pltpu.VMEM, pltpu.HBM))
 
-    def here(*lengths):
-        return pltpu.VMEM(lengths, jnp.float32)
+    def here(*lengths, dtype=jnp.float32):
+        return pltpu.VMEM(lengths, dtype)
 
     def on_chip(x):
         return pltpu.with_memory_space_constraint(x, pltpu.VMEM)
@@ -172,13 +176,17 @@
             out_shape=outs,
             scratch_shapes=scratch,
             compiler_params=pltpu.CompilerParams(vmem_limit_bytes=mib << 20),
-            name=kernel.__name__,
         )(*args)
 
     sent, own, held, tile = call(
         sent_kernel,
         [hbm] * 4,
-        [here(NY, length, width), here(slots, NY * share, width), here(slots, height, width), here(share, width)],
+        [
+            here(NY, length, width),
+            here(2, slots, NY * share, width, dtype=jnp.bfloat16),
+            here(slots, height, width),
+            here(share, width),
+        ],
         24,
         *(
             pltpu.with_memory_space_constraint(x, pltpu.HBM)
@@ -207,15 +215,16 @@
         scratch=[pltpu.SMEM((NY, NC, 1, width), jnp.float32), pltpu.SemaphoreType.DMA],
     )
 
+    parts = lax.all_to_all(summed, BOTH, 0, 0, axis_index_groups=PLANES, tiled=True)
+    total = jnp.sum(parts, axis=0)
+    turned = lax.ppermute(total, BOTH, TURN)
+
+    factor, total = lax.optimization_barrier((factor, total))
     gram, gram_other = call(
         gram_kernel, [vmem], [here(share, width), here(share, width)], 24, on_chip(factor),
         scratch=[pltpu.VMEM((width, width), jnp.float32)],
     )
     gram_odd = lax.ppermute(gram_other, BOTH, TO_ODD)
-
-    parts = lax.all_to_all(summed, BOTH, 0, 0, axis_index_groups=PLANES, tiled=True)
-    total = jnp.sum(parts, axis=0)
-    turned = lax.ppermute(total, BOTH, TURN)
     return jnp.where(core == 0, gram - total, gram_odd - turned)[None]
 
 

time: 85.8 us -> 84.9 us (0.990)
  blocking collectives: 41.6 us -> 63.8 us
  waiting for transfers between devices: 19.4 us -> 8.24 us
  starting transfers between devices: 15.4 us -> 5.8 us
  Pallas kernels: 8.36 us -> 6.14 us
    all_to_all x0 -> x1, blocking collectives: none -> 22.2 us  [on_device(): lax.all_to_all(summed, BOTH, 0, 0, axis_index_groups=PLANES, tiled=True)]
    all_to_all x1 -> x0, waiting for transfers between devices: 11.1 us -> none  [on_device(): lax.all_to_all(summed, BOTH, 0, 0, axis_index_groups=PLANES, tiled=True)]
    all_to_all x1 -> x0, starting transfers between devices: 9.62 us -> none  [on_device(): lax.all_to_all(summed, BOTH, 0, 0, axis_index_groups=PLANES, tiled=True)]
    pallas_call x5, Pallas kernels: 8.36 us -> 6.14 us  [call(): pl.pallas_call(kernel, in_specs=ins, out_specs=[vmem] * len(outs), out_sh...]
  transfers between devices with their start and end apart: 4 -> 3, of which waited for: 3 -> 2; matrix products, arithmetic and copies ran while one was open for 0% -> 0% of each run, Pallas kernels for 1% -> 1%
where the time goes in v5:
time: 84.9 us; the launch traced here: 84.7 us
  blocking collectives  63.8 us (75%)
  waiting for transfers between devices  8.24 us (10%)
  Pallas kernels  6.14 us (7%)
  starting transfers between devices  5.8 us (7%)
    all_to_all x1, blocking collectives, on_device(): lax.all_to_all(payload, BOTH, 0, 0, axis_index_groups=LINES, tiled=True)  41.6 us
    all_to_all x1, blocking collectives, on_device(): lax.all_to_all(summed, BOTH, 0, 0, axis_index_groups=PLANES, tiled=True)  22.2 us
    ppermute x1, waiting for transfers between devices, on_device(): turned = lax.ppermute(total, BOTH, TURN)  6.45 us
    pallas_call x5, Pallas kernels, call(): pl.pallas_call(kernel, in_specs=ins, out_specs=[vmem] * len(outs), out_sh...  6.14 us
    ppermute x1, starting transfers between devices, on_device(): arrived = lax.ppermute(sent, BOTH, PARTNER)  2.58 us
    ppermute x1, starting transfers between devices, on_device(): turned = lax.ppermute(total, BOTH, TURN)  1.92 us
    ppermute x1, waiting for transfers between devices, on_device(): arrived = lax.ppermute(sent, BOTH, PARTNER)  1.79 us
  transfers between devices with their start and end apart: 3, of which 2 were waited for; matrix products, arithmetic and copies ran while one was open for 0% of the time, Pallas kernels for 1%

profile of v5, /device:TPU:9, one launch (start us, length us, event | category | flops | bytes accessed | tf_op | source)
XLA Modules:
  0.0 84.7 jit_solution(5045203759102972546)
XLA Ops:
  0.0 3.4 %shard_map.46 = (f32[8,144,256]{2,1,0:T(8,128)S(1)}, bf16[2,8,128,256]{3,2,1,0:T(8,128)(2,1)S(1)}, f32[8,256,256]{2,1,0:T(8,128)S(1)}, f32[16,256]{1,0:T(8,128)S(1)}) custom-call(s32[8]{0:T(128)} %bitcast.3, f32[8,256,256]{2,1,0:T(8,128)} %left_ref.1, f32[8,256,256]{2,1,0:T(8,128)} %right_ref.1, f32[1,16,256]{2,1,0:T(8,128)} %rows_hbm.1), custom_call_target="tpu_custom_call" | custom-call | tf_op jit(solution)/shard_map/pallas_call | solution.py:172
  3.4 2.6 %collective-permute-start = (f32[8,144,256]{2,1,0:T(8,128)S(1)}, f32[8,144,256]{2,1,0:T(8,128)S(1)}, u32[]{:S(2)}, u32[]{:S(2)}) collective-permute-start(f32[8,144,256]{2,1,0:T(8,128)S(1)} %get-tuple-element.18), channel_id=1, source_target_pairs={{0,32},{1,33},{2,34},{3,35},{4,36},{5,37},{6,38},{7,39},{8,40},{9,... | collective-permute-start | bytes 3538952 | tf_op jit(solution)/shard_map/ppermute | solution.py:203
  6.0 0.7 shard_map.47.kept_ref
  6.7 1.8 %collective-permute-done.arrived_ref = f32[8,144,256]{2,1,0:T(8,128)S(1)} collective-permute-done((f32[8,144,256]{2,1,0:T(8,128)S(1)}, f32[8,144,256]{2,1,0:T(8,128)S(1)}, u32[]{:S(2)}, u32[]{:S(2)}) %collective-permute-start) | collective-permute-done | bytes 1179680 | tf_op jit(solution)/shard_map/ppermute | solution.py:203
  8.5 0.2 shard_map.48
  8.6 41.6 %all_to_all.10.got_ref = f32[8,2,144,256]{3,2,1,0:T(8,128)S(1)} all-to-all(f32[8,2,144,256]{3,2,1,0:T(8,128)S(1)} %shard_map.48), channel_id=1, replica_groups={{0,64,128,192,256,320,384,448},{1,65,129,193,257,321,385,449},{2,66,130..., dimensions={0} | all-to-all | bytes 4718592 | tf_op jit(solution)/shard_map/all_to_all | solution.py:207
  50.3 1.6 %shard_map.49 = (f32[32,16,256]{2,1,0:T(8,128)S(1)}, f32[256,256]{1,0:T(8,128)S(1)}) custom-call(f32[8,2,144,256]{3,2,1,0:T(8,128)S(1)} %all_to_all.10.got_ref), custom_call_target="tpu_custom_call" | custom-call | tf_op jit(solution)/shard_map/pallas_call | solution.py:172
  51.9 22.2 %all_to_all.11 = f32[32,16,256]{2,1,0:T(8,128)S(1)} all-to-all(f32[32,16,256]{2,1,0:T(8,128)S(1)} %get-tuple-element.20), channel_id=1, replica_groups={{0,1,2,3,4,5,6,7,8,9,10,11,12,13,14,15,16,17,18,19,20,21,22,23,24,25,26..., dimensions={0} | all-to-all | bytes 1048576 | tf_op jit(solution)/shard_map/all_to_all | solution.py:218
  74.1 0.3 shard_map.50
  74.4 1.3 %collective-permute-start.1 = (f32[16,256]{1,0:T(8,128)S(1)}, f32[16,256]{1,0:T(8,128)S(1)}, u32[]{:S(2)}, u32[]{:S(2)}) collective-permute-start(f32[16,256]{1,0:T(8,128)S(1)} %get-tuple-element.24), channel_id=1, source_target_pairs={{0,32},{1,33},{2,34},{3,35},{4,36},{5,37},{6,38},{7,39},{8,40},{9,... | collective-permute-start | bytes 49160 | tf_op jit(solution)/shard_map/ppermute | solution.py:227
  75.7 1.9 %collective-permute-start.2 = (f32[16,256]{1,0:T(8,128)S(1)}, f32[16,256]{1,0:T(8,128)S(1)}, u32[]{:S(2)}, u32[]{:S(2)}) collective-permute-start(f32[16,256]{1,0:T(8,128)S(1)} %reduce_sum.9), channel_id=1, source_target_pairs={{32,36},{33,100},{34,164},{35,228},{36,292},{37,356},{38,420},{39,... | collective-permute-start | bytes 49160 | tf_op jit(solution)/shard_map/ppermute | solution.py:220
  77.6 0.0 collective-permute-done.1
  77.7 6.5 %collective-permute-done.2 = f32[16,256]{1,0:T(8,128)S(1)} collective-permute-done((f32[16,256]{1,0:T(8,128)S(1)}, f32[16,256]{1,0:T(8,128)S(1)}, u32[]{:S(2)}, u32[]{:S(2)}) %collective-permute-start.2) | collective-permute-done | bytes 16416 | tf_op jit(solution)/shard_map/ppermute | solution.py:220
  84.1 0.6 select_bitcast_fusion
  (1 shorter events, 0.0 us)
Async XLA Ops:
  3.4 5.0 %collective-permute-start = (f32[8,144,256]{2,1,0:T(8,128)S(1)}, f32[8,144,256]{2,1,0:T(8,128)S(1)}, u32[]{:S(2)}, u32[]{:S(2)}) collective-permute-start(f32[8,144,256]{2,1,0:T(8,128)S(1)} %get-tuple-element.18), channel_id=1, source_target_pairs={{0,32},{1,33},{2,34},{3,35},{4,36},{5,37},{6,38},{7,39},{8,40},{9,... | collective-permute-start | bytes 3538952 | tf_op jit(solution)/shard_map/ppermute | solution.py:203
  74.4 3.2 %collective-permute-start.1 = (f32[16,256]{1,0:T(8,128)S(1)}, f32[16,256]{1,0:T(8,128)S(1)}, u32[]{:S(2)}, u32[]{:S(2)}) collective-permute-start(f32[16,256]{1,0:T(8,128)S(1)} %get-tuple-element.24), channel_id=1, source_target_pairs={{0,32},{1,33},{2,34},{3,35},{4,36},{5,37},{6,38},{7,39},{8,40},{9,... | collective-permute-start | bytes 49160 | tf_op jit(solution)/shard_map/ppermute | solution.py:227
  75.7 8.4 %collective-permute-start.2 = (f32[16,256]{1,0:T(8,128)S(1)}, f32[16,256]{1,0:T(8,128)S(1)}, u32[]{:S(2)}, u32[]{:S(2)}) collective-permute-start(f32[16,256]{1,0:T(8,128)S(1)} %reduce_sum.9), channel_id=1, source_target_pairs={{32,36},{33,100},{34,164},{35,228},{36,292},{37,356},{38,420},{39,... | collective-permute-start | bytes 49160 | tf_op jit(solution)/shard_map/ppermute | solution.py:220
